TPU v7x, 8 devices: a whole 2x2x1 slice. The times are simulated.
8 devices in a mesh: dp: 2 (over z, y), tp: 4 (over x, core).
Axes of the slice: x: 2, y: 2, z: 1, core: 2. Of those that a mesh axis runs over, the one named last changes fastest.
Arguments:
- hidden: bfloat16 [1024, 4096], P('dp'), parts along dimension 0
- w_q: bfloat16 [4096, 4096], P(None, 'tp')
- w_k: bfloat16 [4096, 4096], P(None, 'tp')
- w_v: bfloat16 [4096, 4096], P(None, 'tp')
- w_o: bfloat16 [4096, 4096], P('tp')
- q_norm_w: float32 [4096], P('tp')
- k_norm_w: float32 [4096], P('tp')
- post_norm_w: float32 [4096], replicated
- k_cache: bfloat16 [1024, 32, 32, 128], P('dp', None, 'tp'), parts along dimension 0
- v_cache: bfloat16 [1024, 32, 32, 128], P('dp', None, 'tp'), parts along dimension 0
- positions: int32 [1024], P('dp'), parts along dimension 0
Outputs:
- output 1: bfloat16 [1024, 4096], P('dp'), parts along dimension 0
- output 2: bfloat16 [1024, 32, 32, 128], P('dp', None, 'tp'), parts along dimension 0
- output 3: bfloat16 [1024, 32, 32, 128], P('dp', None, 'tp'), parts along dimension 0
There are 2 independent parts. A program takes and returns all parts, laid end to end along the dimension named above; an argument that names none is the same for every part.
All inputs are finite; a program needn't handle non-finite values.
Results may differ from a plain program's by a relative error of at most 0.010336.
Values are sent between devices in bfloat16 or wider.
A program may use at most 1 GiB of HBM per device.

v0:
```python
import jax
import jax.numpy as jnp
from jax import lax
from jax.sharding import PartitionSpec as P

NORM_EPS = 1e-6
ROPE_BASE = 500000.0


def apply_rope(heads_val, positions):
    head_dim = heads_val.shape[-1]
    half = head_dim // 2
    inv_freq = ROPE_BASE ** (-2.0 * jnp.arange(half, dtype=jnp.float32) / head_dim)
    angles = positions.astype(jnp.float32)[:, None, None] * inv_freq[None, None, :]
    cos_tab = jnp.cos(angles)
    sin_tab = jnp.sin(angles)
    wide = heads_val.astype(jnp.float32)
    first = wide[..., :half]
    second = wide[..., half:]
    return jnp.concatenate([first * cos_tab - second * sin_tab, second * cos_tab + first * sin_tab], axis=-1).astype(jnp.bfloat16)


def write_slot(cache, new_vals, positions):
    slot_ids = jnp.arange(cache.shape[1], dtype=jnp.int32)
    at_slot = (slot_ids[None, :] == positions[:, None])[:, :, None, None]
    return jnp.where(at_slot, new_vals[:, None], cache)


def attend(q_rot, k_new, v_new, positions):
    slot_ids = jnp.arange(k_new.shape[1], dtype=jnp.int32)
    scores = jnp.einsum('bhd,bshd->bhs', q_rot, k_new, preferred_element_type=jnp.float32) * k_new.shape[3] ** -0.5
    valid = (slot_ids[None, :] <= positions[:, None])[:, None, :]
    scores = jnp.where(valid, scores, -1e30)
    probs = jax.nn.softmax(scores, axis=-1).astype(jnp.bfloat16)
    return jnp.einsum('bhs,bshd->bhd', probs, v_new, preferred_element_type=jnp.float32).astype(jnp.bfloat16)


def solution(mesh):
    def local_step(hidden, w_q, w_k, w_v, w_o, q_norm_w, k_norm_w, post_norm_w, k_cache, v_cache, positions):
        n_rows, width = hidden.shape
        local_heads, head_dim = k_cache.shape[2], k_cache.shape[3]
        q_local = jnp.dot(hidden, w_q, preferred_element_type=jnp.float32).astype(jnp.bfloat16).astype(jnp.float32)
        k_local = jnp.dot(hidden, w_k, preferred_element_type=jnp.float32).astype(jnp.bfloat16).astype(jnp.float32)
        v_local = jnp.dot(hidden, w_v, preferred_element_type=jnp.float32).astype(jnp.bfloat16)
        energy = jnp.stack([jnp.sum(q_local * q_local, axis=-1), jnp.sum(k_local * k_local, axis=-1)])
        energy = lax.psum(energy, 'tp')
        inv_rms = lax.rsqrt(energy / width + NORM_EPS)
        q_normed = (q_local * inv_rms[0][:, None] * q_norm_w).astype(jnp.bfloat16).reshape(n_rows, local_heads, head_dim)
        k_normed = (k_local * inv_rms[1][:, None] * k_norm_w).astype(jnp.bfloat16).reshape(n_rows, local_heads, head_dim)
        q_rot = apply_rope(q_normed, positions)
        k_rot = apply_rope(k_normed, positions)
        k_new = write_slot(k_cache, k_rot, positions)
        v_new = write_slot(v_cache, v_local.reshape(n_rows, local_heads, head_dim), positions)
        attn = attend(q_rot, k_new, v_new, positions)
        proj_part = jnp.dot(attn.reshape(n_rows, local_heads * head_dim), w_o, preferred_element_type=jnp.float32).astype(jnp.bfloat16)
        a_out = lax.psum(proj_part, 'tp').astype(jnp.float32)
        inv_out = lax.rsqrt(jnp.mean(a_out * a_out, axis=-1, keepdims=True) + NORM_EPS)
        hidden_out = (hidden.astype(jnp.float32) + a_out * inv_out * post_norm_w).astype(jnp.bfloat16)
        return hidden_out, k_new, v_new

    cache_spec = P('dp', None, 'tp', None)
    return jax.shard_map(local_step, mesh=mesh, in_specs=(P('dp', None), P(None, 'tp'), P(None, 'tp'), P(None, 'tp'), P('tp', None), P('tp'), P('tp'), P(None), cache_spec, cache_spec, P('dp')), out_specs=(P('dp', None), cache_spec, cache_spec), check_vma=False)
```

profile of v0, /device:TPU:0, one launch (start us, length us, event | category | flops | bytes accessed | tf_op | source)
XLA Modules:
  0.0 232.2 jit_solution(13367602963704264669)
XLA Ops:
  7.2 0.0 all-reduce.2.cloned.1.call-start
  7.2 0.7 convert_element_type.69
  7.9 0.7 iota_compare_fusion.1
  8.6 0.2 copy.14
  8.8 0.0 copy-start.1
  8.8 0.0 copy-start.5
  8.8 9.3 %fusion.17 = bf16[64,8,8,128]{3,1,2,0:T(8,128)(2,1)S(1)} fusion(bf16[512,4096]{1,0:T(8,128)(2,1)} %param.11, bf16[4096,1024]{1,0:T(8,128)(2,1)} %param.14), kind=kOutput, calls=%fused_computation.35 | convolution fusion | flops 4295491584 | bytes 13631488 | tf_op jit(solution)/shard_map/dot_general | solution.py:44
  18.1 0.0 slice-start
  18.1 0.3 copy.23
  18.4 0.0 copy-done.1
  18.4 0.0 copy-done.5
  18.4 0.0 slice-start.1
  18.4 4.6 %fusion.10 = (f32[512]{0:T(512)S(1)}, bf16[512,1024]{1,0:T(8,128)(2,1)S(1)}) fusion(bf16[512,4096]{1,0:T(8,128)(2,1)S(1)} %copy-done.1, bf16[4096,1024]{1,0:T(8,128)(2,1)S(1)} %copy-done.5), kind=kOutput, calls=%fused_computation.19 | convolution fusion | flops 4297063936 | bytes 13633536 | tf_op jit(solution)/shard_map/dot_general | solution.py:42
  23.0 0.0 slice-done
  23.0 0.0 slice-done.1
  23.1 0.0 copy-start.3
  23.1 4.6 %fusion.13 = (f32[512]{0:T(512)S(1)}, bf16[512,1024]{1,0:T(8,128)(2,1)S(1)}) fusion(bf16[512,4096]{1,0:T(8,128)(2,1)S(1)} %copy-done.1, bf16[4096,1024]{1,0:T(8,128)(2,1)S(1)} %bitcast.50), kind=kOutput, calls=%fused_computation.22 | convolution fusion | flops 4297063936 | bytes 13633536 | tf_op jit(solution)/shard_map/dot_general | solution.py:43
  27.7 0.0 copy-start.4
  27.7 8.8 %psum.14 = f32[2,512]{1,0:T(2,128)S(1)} all-reduce(f32[2,512]{1,0:T(2,128)S(1)} %pad_maximum_fusion.1), channel_id=1, replica_groups=mesh['dp'=2,'tp'=4] {'tp'}, use_global_device_ids=true, to_apply=%region_2.0 | all-reduce | flops 1024 | bytes 8192 | tf_op jit(solution)/shard_map/psum | solution.py:46
  36.5 0.0 copy-done.3
  36.5 0.3 convert_bitcast_fusion
  36.8 0.5 copy.22
  37.2 0.0 copy-done.4
  37.3 0.3 convert_bitcast_fusion.1
  37.5 0.5 copy.21
  38.0 1.0 multiply_cosine_fusion
  39.0 1.5 subtract_convert_fusion.1
  40.5 0.6 maximum_bitcast_fusion
  41.1 0.6 pad_maximum_fusion
  41.7 44.3 %broadcast_select_fusion = (bf16[512,32,8,128]{3,2,1,0:T(8,128)(2,1)}, bf16[512,32,8,128]{3,2,1,0:T(8,128)(2,1)}) fusion(bf16[512,32,8,128]{3,2,1,0:T(8,128)(2,1)} %param.20, pred[512,32]{1,0:T(8,128)(4,1)S(1)} %copy.14, bf16[512,8,128]{2,1,0:T(8,128)(2,1)S(1)} %bitcast.42, bf16[512,32,8,128]{3,2,1,0:T(8,128)(2,1)} %param.19, ...), kind=kLoop, calls=%fused_computation.6 | loop fusion | flops 33554432 | bytes 136331264 | tf_op jit(solution)/shard_map/jit(_where)/select_n | solution.py:26
  86.0 21.1 %fusion.4 = f32[512,8,1,32]{3,2,1,0:T(1,128)S(1)} fusion(bf16[512,32,8,128]{3,2,1,0:T(8,128)(2,1)} %get-tuple-element.10, bf16[512,8,128,1]{2,1,0,3:T(8,128)(2,1)S(1)} %maximum_bitcast_fusion), kind=kOutput, calls=%fused_computation.4 | convolution fusion | flops 33554432 | bytes 35127296 | tf_op jit(solution)/shard_map/bhd,bshd->bhs/dot_general | solution.py:31
  107.1 2.3 %copy.17 = f32[512,8,1,32]{0,3,1,2:T(8,128)S(1)} copy(f32[512,8,1,32]{3,2,1,0:T(1,128)S(1)} %fusion.4) | data formatting | bytes 1048576 | tf_op jit(solution)/shard_map/bhd,bshd->bhs/dot_general | solution.py:31
  109.5 0.2 fusion.22
  109.7 1.8 copy.18
  111.5 14.4 %fusion.2 = f32[512,8,1,128]{3,2,1,0:T(1,128)S(1)} fusion(bf16[512,8,32,1]{2,3,1,0:T(2,128)(2,1)S(1)} %copy.18, bf16[512,32,8,128]{3,2,1,0:T(8,128)(2,1)} %get-tuple-element.9), kind=kOutput, calls=%fused_computation.2 | convolution fusion | flops 33554432 | bytes 35913728 | tf_op jit(solution)/shard_map/bhs,bshd->bhd/dot_general | solution.py:35
  126.0 0.1 convert_element_type.75
  126.1 9.4 %convolution_convert_fusion = bf16[512,4096]{1,0:T(8,128)(2,1)} fusion(bf16[1024,4096]{1,0:T(8,128)(2,1)} %param.15, bf16[64,8,8,128]{3,2,1,0:T(8,128)(2,1)S(1)} %bitcast.44), kind=kOutput, calls=%fused_computation.14 | convolution fusion | flops 4297064448 | bytes 13631488 | tf_op jit(solution)/shard_map/dot_general | solution.py:55
  135.5 0.0 copy-start.2
  135.5 0.0 all-reduce.2.cloned.1.call-update
  135.6 79.9 %all-reduce.2.cloned.1.call-done = bf16[512,4096]{1,0:T(8,128)(2,1)} async-done(((bf16[512,4096]{1,0:T(8,128)(2,1)}), bf16[512,4096]{1,0:T(8,128)(2,1)}) %all-reduce.2.cloned.1.call-update) | async-done | bytes 4194320 | tf_op jit(solution)/shard_map/psum | solution.py:56
  215.5 0.0 copy-start
  215.5 3.2 %fusion.6 = f32[512]{0:T(512)S(1)} fusion(bf16[512,4096]{1,0:T(8,128)(2,1)} %all-reduce.2.cloned.1.call-done), kind=kLoop, calls=%fused_computation.10 | loop fusion | flops 6290944 | bytes 4196352 | tf_op jit(solution)/shard_map/reduce_sum | solution.py:57
  218.8 0.0 copy-done.2
  218.8 0.2 copy-done
  219.0 6.4 %fusion.9 = bf16[512,4096]{1,0:T(8,128)(2,1)} fusion(bf16[512,4096]{1,0:T(8,128)(2,1)S(1)} %copy-done, bf16[512,4096]{1,0:T(8,128)(2,1)} %param.11, f32[4096]{0:T(1024)S(1)} %copy-done.2, f32[512]{0:T(512)S(1)} %add_rsqrt_fusion.1), kind=kLoop, calls=%fused_computation.13 | loop fusion | flops 12582912 | bytes 12601344 | tf_op jit(solution)/shard_map/convert_element_type | solution.py:58
  (6 shorter events, 0.0 us)
Async XLA Ops:
  7.2 208.4 %all-reduce.2.cloned.1.call-start = ((), (), s32[]{:S(2)}) async-start(), calls=%async_computation | async-start | bytes 8388608 | tf_op jit(solution)/shard_map/psum | solution.py:56
  8.8 9.6 %copy-start.1 = (bf16[512,4096]{1,0:T(8,128)(2,1)S(1)}, bf16[512,4096]{1,0:T(8,128)(2,1)}, u32[]{:S(2)}) copy-start(bf16[512,4096]{1,0:T(8,128)(2,1)} %param.11) | copy-start | bytes 12582916
  8.8 9.6 %copy-start.5 = (bf16[4096,1024]{1,0:T(8,128)(2,1)S(1)}, bf16[4096,1024]{1,0:T(8,128)(2,1)}, u32[]{:S(2)}) copy-start(bf16[4096,1024]{1,0:T(8,128)(2,1)} %param.12) | copy-start | bytes 25165828
  18.1 4.9 %slice-start = ((s8[8388608]{0:T(1024)(128)(4,1)}), s8[4194304]{0:T(1024)(128)(4,1)S(1)}, s32[]{:S(2)}) async-start(s8[8388608]{0:T(1024)(128)(4,1)} %bitcast.49), calls=%async_computation.1 | async-start | bytes 8388608
  18.4 4.6 %slice-start.1 = ((s8[8388608]{0:T(1024)(128)(4,1)}), s8[4194304]{0:T(1024)(128)(4,1)S(1)}, s32[]{:S(2)}) async-start(s8[8388608]{0:T(1024)(128)(4,1)} %bitcast.49), calls=%async_computation.2 | async-start | bytes 8388608
  23.1 13.4 %copy-start.3 = (f32[1024]{0:T(1024)S(1)}, f32[1024]{0:T(1024)}, u32[]{:S(2)}) copy-start(f32[1024]{0:T(1024)} %param.17) | copy-start | bytes 12292
  27.7 9.6 %copy-start.4 = (f32[1024]{0:T(1024)S(1)}, f32[1024]{0:T(1024)}, u32[]{:S(2)}) copy-start(f32[1024]{0:T(1024)} %param.16) | copy-start | bytes 12292
  135.5 83.2 %copy-start.2 = (f32[4096]{0:T(1024)S(1)}, f32[4096]{0:T(1024)}, u32[]{:S(2)}) copy-start(f32[4096]{0:T(1024)} %param.18) | copy-start | bytes 49156
  215.5 3.4 %copy-start = (bf16[512,4096]{1,0:T(8,128)(2,1)S(1)}, bf16[512,4096]{1,0:T(8,128)(2,1)}, u32[]{:S(2)}) copy-start(bf16[512,4096]{1,0:T(8,128)(2,1)} %all-reduce.2.cloned.1.call-done) | copy-start | bytes 12582916
Sparse Core Ops, SparseCore 0:
  135.7 79.7 all-reduce.1
where the time goes:
time: 232 us
  waiting for transfers between devices  80 us (34%)
  matrix products  63.5 us (27%)
  other arithmetic  59.9 us (26%)
  between operations  14.3 us (6%)
  blocking collectives  8.76 us (4%)
  local copies, waits for them, and re-layouts  5.81 us (3%)
    psum x1, waiting for transfers between devices, local_step(): a_out = lax.psum(proj_part, 'tp').astype(jnp.float32)  79.9 us
    select_n x1, other arithmetic, write_slot(): return jnp.where(at_slot, new_vals[:, None], cache)  44.3 us
    dot_general x1, matrix products, attend(): jnp.einsum('bhd,bshd->bhs', q_rot, k_new, preferred_element_type=jnp.floa...  21.1 us
    dot_general x1, matrix products, attend(): jnp.einsum('bhs,bshd->bhd', probs, v_new, preferred_element_type=jnp.floa...  14.4 us
    dot_general x1, matrix products, local_step(): jnp.dot(attn.reshape(n_rows, local_heads * head_dim), w_o, preferred_elem...  9.43 us
    dot_general x1, matrix products, local_step(): jnp.dot(hidden, w_v, preferred_element_type=jnp.float32)  9.28 us
    psum x1, blocking collectives, local_step(): energy = lax.psum(energy, 'tp')  8.76 us
    convert_element_type x1, other arithmetic, local_step(): (hidden.astype(jnp.float32) + a_out * inv_out * post_norm_w).astype(jnp.b...  6.36 us
  transfers between devices with their start and end apart: 1, of which 1 were waited for; matrix products, arithmetic and copies ran while one was open for 0% of the time, Pallas kernels for 0%

commit v1 on v0

v1 whole, which is shorter than its diff:
```python
import functools

import jax
import jax.numpy as jnp
from jax import lax
from jax.experimental import pallas as pl
from jax.experimental.pallas import tpu as pltpu
from jax.sharding import PartitionSpec as P


NORM_EPS = 1e-6
ROPE_BASE = 500000.0
CHUNKS = (64,) * 8
BLOCK = 8
DEPTH = 6
AHEAD = 3
FINAL_ROWS = 16
PARTNER = [(0, 1), (1, 0), (2, 3), (3, 2)]
PEER = [(0, 2), (2, 0), (1, 3), (3, 1)]

VMEM = pl.BlockSpec(memory_space=pltpu.VMEM)
SMEM = pl.BlockSpec(memory_space=pltpu.SMEM)
ANY = pl.BlockSpec(memory_space=pl.ANY)


def attend_kernel(row0, rows, *refs):
    pos, core, q, kn, vn, wo, kc, vc = refs[:8]
    ko, vo, keep, send, kbuf, vbuf, o_f32, o_bf, isem, osem = refs[-10:]
    blocks = rows // BLOCK
    heads, dim = q.shape[1], q.shape[2]
    slots = kc.shape[1]

    def copies_in(j, s):
        at = pl.ds(row0 + j * BLOCK, BLOCK)
        return (pltpu.make_async_copy(kc.at[at], kbuf.at[s], isem.at[s, 0]),
                pltpu.make_async_copy(vc.at[at], vbuf.at[s], isem.at[s, 1]))

    def copies_out(j, s):
        at = pl.ds(row0 + j * BLOCK, BLOCK)
        return (pltpu.make_async_copy(kbuf.at[s], ko.at[at], osem.at[s, 0]),
                pltpu.make_async_copy(vbuf.at[s], vo.at[at], osem.at[s, 1]))

    for j in range(min(AHEAD, blocks)):
        for c in copies_in(j, j):
            c.start()

    lane = lax.broadcasted_iota(jnp.int32, (heads, slots * heads), 1)
    head = lax.broadcasted_iota(jnp.int32, (heads, slots * heads), 0)
    slot_of = jnp.where(lax.rem(lane, heads) == head, lax.div(lane, heads), slots)

    def step(i, carry):
        s = lax.rem(i, DEPTH)
        nxt = i + AHEAD

        @pl.when(nxt < blocks)
        def _():
            @pl.when(nxt >= DEPTH)
            def _():
                for c in copies_out(nxt - DEPTH, lax.rem(nxt, DEPTH)):
                    c.wait()

            for c in copies_in(nxt, lax.rem(nxt, DEPTH)):
                c.start()

        for c in copies_in(i, s):
            c.wait()
        base = i * BLOCK
        for r in range(BLOCK):
            p = pos[row0 + base + r]
            kbuf[s, r, p] = kn[row0 + base + r]
            vbuf[s, r, p] = vn[row0 + base + r]
        for r in range(BLOCK):
            p = pos[row0 + base + r]
            k = kbuf[s, r].reshape(slots * heads, dim)
            v = vbuf[s, r].reshape(slots * heads, dim)
            score = lax.dot_general(q[row0 + base + r], k, (((1,), (1,)), ((), ())), preferred_element_type=jnp.float32)
            score = jnp.where(slot_of <= p, score * dim ** -0.5, -1e30)
            e = jnp.exp(score - jnp.max(score, axis=-1, keepdims=True))
            prob = (e / jnp.sum(e, axis=-1, keepdims=True)).astype(jnp.bfloat16)
            o_f32[pl.ds((base + r) * heads, heads)] = jnp.dot(prob, v, preferred_element_type=jnp.float32)
        for c in copies_out(i, s):
            c.start()
        return carry

    lax.fori_loop(0, blocks, step, 0)
    for h in range(heads):
        o_bf[:, h * dim:(h + 1) * dim] = o_f32[pl.ds(h, rows, stride=heads), :].astype(jnp.bfloat16)
    half = rows // 2
    for which, out in ((core[0], keep), (1 - core[0], send)):
        o = o_bf[pl.ds(pl.multiple_of(which * half, 16), half), :]
        for n in range(0, wo.shape[1], 512):
            out[:, n:n + 512] = jnp.dot(o, wo[:, n:n + 512], preferred_element_type=jnp.float32).astype(jnp.bfloat16)
    for j in range(max(0, blocks - DEPTH), blocks):
        for c in copies_out(j, j % DEPTH):
            c.wait()


def attend(row0, rows, pos, core, q, kn, vn, wo, kc, vc, prev):
    width = wo.shape[1]
    args = (pos, core, q, kn, vn, wo, kc, vc) + prev
    share = jax.ShapeDtypeStruct((rows // 2, width), jnp.bfloat16)
    return pl.pallas_call(
        functools.partial(attend_kernel, row0, rows),
        out_shape=(jax.ShapeDtypeStruct(kc.shape, kc.dtype), jax.ShapeDtypeStruct(vc.shape, vc.dtype), share, share),
        in_specs=[SMEM, SMEM, VMEM, VMEM, VMEM, VMEM, ANY, ANY] + [ANY] * len(prev),
        out_specs=(ANY, ANY, VMEM, VMEM),
        input_output_aliases={8: 0, 9: 1} if prev else {},
        scratch_shapes=[
            pltpu.VMEM((DEPTH, BLOCK) + kc.shape[1:], kc.dtype),
            pltpu.VMEM((DEPTH, BLOCK) + vc.shape[1:], vc.dtype),
            pltpu.VMEM((rows * q.shape[1], q.shape[2]), jnp.float32),
            pltpu.VMEM((rows, q.shape[1] * q.shape[2]), jnp.bfloat16),
            pltpu.SemaphoreType.DMA((DEPTH, 2)),
            pltpu.SemaphoreType.DMA((DEPTH, 2)),
        ],
        compiler_params=pltpu.CompilerParams(vmem_limit_bytes=32 * 2 ** 20),
        cost_estimate=pl.CostEstimate(flops=rows * 75_000_000, bytes_accessed=rows * 4 * 65536, transcendentals=0),
        name='attend',
    )(*args)


def final_kernel(core, hid, own, peer, own2, peer2, gain, *rest):
    out = rest[-1]
    j = pl.program_id(0)

    def emit(a, b):
        total = a[...].astype(jnp.float32) + b[...].astype(jnp.float32)
        inv = lax.rsqrt(jnp.mean(total * total, axis=-1, keepdims=True) + NORM_EPS)
        out[...] = (hid[...].astype(jnp.float32) + total * inv * gain[...]).astype(jnp.bfloat16)

    @pl.when(j == 0)
    def _():
        emit(own, peer)

    @pl.when(j == 1)
    def _():
        emit(own2, peer2)


def finish(row0, rows, core, hidden, own, peer, own2, peer2, gain, prev):
    width = hidden.shape[1]
    blocks = rows // 2 // FINAL_ROWS
    first = row0 // FINAL_ROWS

    def place(j, b, core):
        which = core[0] + j - 2 * core[0] * j
        return (first + which * blocks + b, 0)

    mine = pl.BlockSpec((FINAL_ROWS, width), lambda j, b, core: (b + j * (blocks - 1 - b), 0))
    other = pl.BlockSpec((FINAL_ROWS, width), lambda j, b, core: (b * j, 0))
    return pl.pallas_call(
        final_kernel,
        out_shape=jax.ShapeDtypeStruct(hidden.shape, hidden.dtype),
        grid_spec=pltpu.PrefetchScalarGridSpec(
            num_scalar_prefetch=1,
            grid=(2, blocks),
            in_specs=[pl.BlockSpec((FINAL_ROWS, width), place), mine, mine, other, other,
                      pl.BlockSpec((1, width), lambda j, b, core: (0, 0))] + [ANY] * len(prev),
            out_specs=pl.BlockSpec((FINAL_ROWS, width), place),
        ),
        input_output_aliases={7: 0} if prev else {},
        compiler_params=pltpu.CompilerParams(vmem_limit_bytes=8 * 2 ** 20),
        cost_estimate=pl.CostEstimate(flops=rows * 8_000_000, bytes_accessed=rows * 32768, transcendentals=0),
        name='finish',
    )(core, hidden, own, peer, own2, peer2, gain, *prev)


def apply_rope(heads_val, positions):
    head_dim = heads_val.shape[-1]
    half = head_dim // 2
    inv_freq = ROPE_BASE ** (-2.0 * jnp.arange(half, dtype=jnp.float32) / head_dim)
    angles = positions.astype(jnp.float32)[:, None, None] * inv_freq[None, None, :]
    cos_tab = jnp.cos(angles)
    sin_tab = jnp.sin(angles)
    wide = heads_val.astype(jnp.float32)
    first = wide[..., :half]
    second = wide[..., half:]
    return jnp.concatenate([first * cos_tab - second * sin_tab, second * cos_tab + first * sin_tab], axis=-1).astype(jnp.bfloat16)


def solution(mesh):
    def local_step(hidden, w_q, w_k, w_v, w_o, q_norm_w, k_norm_w, post_norm_w, k_cache, v_cache, positions):
        n_rows, width = hidden.shape
        local_heads, head_dim = k_cache.shape[2], k_cache.shape[3]
        q_local = jnp.dot(hidden, w_q, preferred_element_type=jnp.float32).astype(jnp.bfloat16).astype(jnp.float32)
        k_local = jnp.dot(hidden, w_k, preferred_element_type=jnp.float32).astype(jnp.bfloat16).astype(jnp.float32)
        v_local = jnp.dot(hidden, w_v, preferred_element_type=jnp.float32).astype(jnp.bfloat16)
        energy = jnp.stack([jnp.sum(q_local * q_local, axis=-1), jnp.sum(k_local * k_local, axis=-1)])
        energy = lax.psum(energy, 'tp')
        inv_rms = lax.rsqrt(energy / width + NORM_EPS)
        q_normed = (q_local * inv_rms[0][:, None] * q_norm_w).astype(jnp.bfloat16).reshape(n_rows, local_heads, head_dim)
        k_normed = (k_local * inv_rms[1][:, None] * k_norm_w).astype(jnp.bfloat16).reshape(n_rows, local_heads, head_dim)
        q_rot = apply_rope(q_normed, positions)
        k_rot = apply_rope(k_normed, positions)
        v_new = v_local.reshape(n_rows, local_heads, head_dim)
        core = jnp.reshape(lax.rem(lax.axis_index('tp'), 2), (1,)).astype(jnp.int32)
        gain = post_norm_w.reshape(1, width)

        caches, out, row0 = (), (), 0
        for rows in CHUNKS:
            k_out, v_out, keep, send = attend(row0, rows, positions, core, q_rot, k_rot, v_new, w_o, k_cache, v_cache, caches)
            caches = (k_out, v_out)
            got = lax.ppermute(send, 'tp', PARTNER)
            own = (keep.astype(jnp.float32) + got.astype(jnp.float32)).astype(jnp.bfloat16)
            peer = lax.ppermute(own, 'tp', PEER)
            own2 = lax.ppermute(own, 'tp', PARTNER)
            peer2 = lax.ppermute(peer, 'tp', PARTNER)
            out = (finish(row0, rows, core, hidden, own, peer, own2, peer2, gain, out),)
            row0 += rows
        return out[0], caches[0], caches[1]

    cache_spec = P('dp', None, 'tp', None)
    return jax.shard_map(local_step, mesh=mesh, in_specs=(P('dp', None), P(None, 'tp'), P(None, 'tp'), P(None, 'tp'), P('tp', None), P('tp'), P('tp'), P(None), cache_spec, cache_spec, P('dp')), out_specs=(P('dp', None), cache_spec, cache_spec), check_vma=False)
```

time: 232 us -> 316 us (1.36)
  Pallas kernels: 0 us -> 226 us
  other arithmetic: 59.9 us -> 4.98 us
  matrix products: 63.5 us -> 18.5 us
  waiting for transfers between devices: 80 us -> 41.4 us
  between operations: 14.3 us -> 1.03 us
  starting transfers between devices: 0.04 us -> 10.7 us
    pallas_call x0 -> x16, Pallas kernels: none -> 226 us  [the longest x8 211 us: attend(): pl.pallas_call(functools.partial(attend_kernel, row0, rows), out_shape=(j...]
    psum x1 -> x0, waiting for transfers between devices: 79.9 us -> none  [local_step(): a_out = lax.psum(proj_part, 'tp').astype(jnp.float32)]
    dot_general x3 -> x0, matrix products: 45 us -> none  [the longest x1 21.1 us: attend(): jnp.einsum('bhd,bshd->bhs', q_rot, k_new, preferred_element_type=jnp.floa...]
    select_n x1 -> x0, other arithmetic: 44.3 us -> none  [write_slot(): return jnp.where(at_slot, new_vals[:, None], cache)]
    ppermute x0 -> x32, waiting for transfers between devices: none -> 41.4 us  [the longest x8 39.9 us: local_step(): peer = lax.ppermute(own, 'tp', PEER)]
    ppermute x0 -> x32, starting transfers between devices: none -> 10.7 us  [the longest x8 6.7 us: local_step(): peer = lax.ppermute(own, 'tp', PEER)]
    convert_element_type x2 -> x8, other arithmetic: 6.47 us -> 0.5 us  [local_step(): (keep.astype(jnp.float32) + got.astype(jnp.float32)).astype(jnp.bfloat16)]
    dot_general x1, matrix products: 9.28 us -> 4.5 us  [local_step(): jnp.dot(hidden, w_v, preferred_element_type=jnp.float32)]
  transfers between devices with their start and end apart: 1 -> 32, of which waited for: 1 -> 13; matrix products, arithmetic and copies ran while one was open for 0% -> 0% of each run, Pallas kernels for 0% -> 4%
where the time goes in v1:
time: 316 us
  Pallas kernels  226 us (72%)
  waiting for transfers between devices  41.4 us (13%)
  matrix products  18.5 us (6%)
  starting transfers between devices  10.7 us (3%)
  blocking collectives  8.72 us (3%)
  local copies, waits for them, and re-layouts  4.99 us (2%)
  other arithmetic  4.98 us (2%)
    pallas_call x8, Pallas kernels, attend(): pl.pallas_call(functools.partial(attend_kernel, row0, rows), out_shape=(j...  211 us
    ppermute x8, waiting for transfers between devices, local_step(): peer = lax.ppermute(own, 'tp', PEER)  39.9 us
    pallas_call x8, Pallas kernels, finish(): pl.pallas_call(final_kernel, out_shape=jax.ShapeDtypeStruct(hidden.shape,...  15 us
    dot_general x1, matrix products, local_step(): jnp.dot(hidden, w_k, preferred_element_type=jnp.float32)  9.36 us
    psum x1, blocking collectives, local_step(): energy = lax.psum(energy, 'tp')  8.72 us
    ppermute x8, starting transfers between devices, local_step(): peer = lax.ppermute(own, 'tp', PEER)  6.7 us
  transfers between devices with their start and end apart: 32, of which 13 were waited for; matrix products, arithmetic and copies ran while one was open for 0% of the time, Pallas kernels for 4%

profile of v1, /device:TPU:0, one launch (start us, length us, event | category | flops | bytes accessed | tf_op | source)
XLA Modules:
  0.0 316.2 jit_solution(14928798962833056563)
XLA Ops:
  0.7 9.4 %fusion.3 = (f32[512]{0:T(512)S(1)}, bf16[512,1024]{1,0:T(8,128)(2,1)S(1)}) fusion(bf16[512,4096]{1,0:T(8,128)(2,1)} %hid.15, bf16[4096,1024]{1,0:T(8,128)(2,1)} %param.13), kind=kOutput, calls=%fused_computation.7 | convolution fusion | flops 4297063936 | bytes 13633536 | tf_op jit(solution)/shard_map/dot_general | solution.py:186
  10.1 4.6 %fusion = (f32[512]{0:T(512)S(1)}, bf16[512,1024]{1,0:T(8,128)(2,1)S(1)}) fusion(bf16[512,4096]{1,0:T(8,128)(2,1)S(1)} %copy-done, bf16[4096,1024]{1,0:T(8,128)(2,1)S(1)} %copy-done.7), kind=kOutput, calls=%fused_computation.4 | convolution fusion | flops 4297063936 | bytes 13633536 | tf_op jit(solution)/shard_map/dot_general | solution.py:185
  14.7 8.7 %psum.7 = f32[2,512]{1,0:T(2,128)S(1)} all-reduce(f32[2,512]{1,0:T(2,128)S(1)} %pad_maximum_fusion.2), channel_id=1, replica_groups=mesh['dp'=2,'tp'=4] {'tp'}, use_global_device_ids=true, to_apply=%region_2.0 | all-reduce | flops 1024 | bytes 8192 | tf_op jit(solution)/shard_map/psum | solution.py:189
  23.5 0.3 convert_bitcast_fusion
  23.8 0.5 copy.36
  24.3 0.3 convert_bitcast_fusion.1
  24.6 0.5 copy.35
  25.1 1.8 copy-done.8
  26.9 1.4 copy-done.1
  28.2 4.5 %fusion.6 = bf16[64,8,8,128]{3,1,2,0:T(8,128)(2,1)S(1)} fusion(bf16[512,4096]{1,0:T(8,128)(2,1)S(1)} %copy-done.1, bf16[4096,1024]{1,0:T(8,128)(2,1)S(1)} %copy-done.8), kind=kOutput, calls=%fused_computation.19 | convolution fusion | flops 4295491584 | bytes 13631488 | tf_op jit(solution)/shard_map/dot_general | solution.py:187
  32.8 0.3 copy.37
  33.0 1.0 multiply_cosine_fusion
  34.0 1.8 subtract_convert_fusion
  35.8 1.2 pad_maximum_fusion
  37.0 0.5 slice-done.1
  37.5 26.4 %attend.8 = (bf16[512,32,8,128]{3,2,1,0:T(8,128)(2,1)}, bf16[512,32,8,128]{3,2,1,0:T(8,128)(2,1)}, bf16[32,4096]{1,0:T(8,128)(2,1)S(1)}, bf16[32,4096]{1,0:T(8,128)(2,1)S(1)}) custom-call(s32[512]{0:T(512)S(1)} %copy-done.4, s32[1]{0:T(128)} %bitcast.refs_1_.core, bf16[512,8,128]{2,1,0:T(8,128)(2,1)S(1)} %get-tuple-element.81.refs_2_, ...), custom_call_target="tpu_custom_call" | custom-call | flops 4800000000 | bytes 16777216 | tf_op jit(solution)/shard_map/attend/pallas_call | solution.py:102
  63.9 26.4 %attend.9 = (bf16[512,32,8,128]{3,2,1,0:T(8,128)(2,1)}, bf16[512,32,8,128]{3,2,1,0:T(8,128)(2,1)}, bf16[32,4096]{1,0:T(8,128)(2,1)S(1)}, bf16[32,4096]{1,0:T(8,128)(2,1)S(1)}) custom-call(s32[512]{0:T(512)S(1)} %copy-done.4, s32[1]{0:T(128)} %bitcast.refs_1_.core, ...), custom_call_target="tpu_custom_call", output_to_operand_aliasing={{0}: (8, {}), {1}: (9, {})} | custom-call | flops 4800000000 | bytes 16777216 | tf_op jit(solution)/shard_map/attend/pallas_call | solution.py:102
  90.2 26.4 %attend.10 = (bf16[512,32,8,128]{3,2,1,0:T(8,128)(2,1)}, bf16[512,32,8,128]{3,2,1,0:T(8,128)(2,1)}, bf16[32,4096]{1,0:T(8,128)(2,1)S(1)}, bf16[32,4096]{1,0:T(8,128)(2,1)S(1)}) custom-call(s32[512]{0:T(512)S(1)} %copy-done.4, s32[1]{0:T(128)} %bitcast.refs_1_.core, ...), custom_call_target="tpu_custom_call", output_to_operand_aliasing={{0}: (8, {}), {1}: (9, {})} | custom-call | flops 4800000000 | bytes 16777216 | tf_op jit(solution)/shard_map/attend/pallas_call | solution.py:102
  116.6 26.4 %attend.11 = (bf16[512,32,8,128]{3,2,1,0:T(8,128)(2,1)}, bf16[512,32,8,128]{3,2,1,0:T(8,128)(2,1)}, bf16[32,4096]{1,0:T(8,128)(2,1)S(1)}, bf16[32,4096]{1,0:T(8,128)(2,1)S(1)}) custom-call(s32[512]{0:T(512)S(1)} %copy-done.4, s32[1]{0:T(128)} %bitcast.refs_1_.core, ...), custom_call_target="tpu_custom_call", output_to_operand_aliasing={{0}: (8, {}), {1}: (9, {})} | custom-call | flops 4800000000 | bytes 16777216 | tf_op jit(solution)/shard_map/attend/pallas_call | solution.py:102
  143.0 26.4 %attend.12 = (bf16[512,32,8,128]{3,2,1,0:T(8,128)(2,1)}, bf16[512,32,8,128]{3,2,1,0:T(8,128)(2,1)}, bf16[32,4096]{1,0:T(8,128)(2,1)S(1)}, bf16[32,4096]{1,0:T(8,128)(2,1)S(1)}) custom-call(s32[512]{0:T(512)S(1)} %copy-done.4, s32[1]{0:T(128)} %bitcast.refs_1_.core, ...), custom_call_target="tpu_custom_call", output_to_operand_aliasing={{0}: (8, {}), {1}: (9, {})} | custom-call | flops 4800000000 | bytes 16777216 | tf_op jit(solution)/shard_map/attend/pallas_call | solution.py:102
  169.4 26.4 %attend.13 = (bf16[512,32,8,128]{3,2,1,0:T(8,128)(2,1)}, bf16[512,32,8,128]{3,2,1,0:T(8,128)(2,1)}, bf16[32,4096]{1,0:T(8,128)(2,1)S(1)}, bf16[32,4096]{1,0:T(8,128)(2,1)S(1)}) custom-call(s32[512]{0:T(512)S(1)} %copy-done.4, s32[1]{0:T(128)} %bitcast.refs_1_.core, ...), custom_call_target="tpu_custom_call", output_to_operand_aliasing={{0}: (8, {}), {1}: (9, {})} | custom-call | flops 4800000000 | bytes 16777216 | tf_op jit(solution)/shard_map/attend/pallas_call | solution.py:102
  195.7 26.4 %attend.14 = (bf16[512,32,8,128]{3,2,1,0:T(8,128)(2,1)}, bf16[512,32,8,128]{3,2,1,0:T(8,128)(2,1)}, bf16[32,4096]{1,0:T(8,128)(2,1)S(1)}, bf16[32,4096]{1,0:T(8,128)(2,1)S(1)}) custom-call(s32[512]{0:T(512)S(1)} %copy-done.4, s32[1]{0:T(128)} %bitcast.refs_1_.core, ...), custom_call_target="tpu_custom_call", output_to_operand_aliasing={{0}: (8, {}), {1}: (9, {})} | custom-call | flops 4800000000 | bytes 16777216 | tf_op jit(solution)/shard_map/attend/pallas_call | solution.py:102
  222.1 26.4 %attend.15 = (bf16[512,32,8,128]{3,2,1,0:T(8,128)(2,1)}, bf16[512,32,8,128]{3,2,1,0:T(8,128)(2,1)}, bf16[32,4096]{1,0:T(8,128)(2,1)S(1)}, bf16[32,4096]{1,0:T(8,128)(2,1)S(1)}) custom-call(s32[512]{0:T(512)S(1)} %copy-done.4, s32[1]{0:T(128)} %bitcast.refs_1_.core, ...), custom_call_target="tpu_custom_call", output_to_operand_aliasing={{0}: (8, {}), {1}: (9, {})} | custom-call | flops 4800000000 | bytes 16777216 | tf_op jit(solution)/shard_map/attend/pallas_call | solution.py:102
  248.6 0.5 collective-permute-start.4
  249.1 0.5 collective-permute-start.12
  249.6 0.5 collective-permute-done
  250.1 0.1 collective-permute-start.20
  250.3 0.2 collective-permute-done.4
  250.5 0.2 collective-permute-start.24
  250.8 0.1 collective-permute-done.8
  250.8 0.2 collective-permute-start.28
  251.1 0.1 collective-permute-done.12
  251.2 0.4 collective-permute-start.9
  251.7 0.1 collective-permute-start.10
  251.8 0.2 collective-permute-done.20
  252.0 1.5 collective-permute-start.1
  253.5 0.6 collective-permute-start.5
  254.1 1.5 collective-permute-start.13
  255.6 10.4 %collective-permute-done.1.peer = bf16[32,4096]{1,0:T(8,128)(2,1)S(1)} collective-permute-done((bf16[32,4096]{1,0:T(8,128)(2,1)S(1)}, bf16[32,4096]{1,0:T(8,128)(2,1)S(1)}, u32[]{:S(2)}, u32[]{:S(2)}) %collective-permute-start.1) | collective-permute-done | bytes 262176 | tf_op jit(solution)/shard_map/ppermute | solution.py:205
  266.0 5.6 %collective-permute-done.5.peer = bf16[32,4096]{1,0:T(8,128)(2,1)S(1)} collective-permute-done((bf16[32,4096]{1,0:T(8,128)(2,1)S(1)}, bf16[32,4096]{1,0:T(8,128)(2,1)S(1)}, u32[]{:S(2)}, u32[]{:S(2)}) %collective-permute-start.5) | collective-permute-done | bytes 262176 | tf_op jit(solution)/shard_map/ppermute | solution.py:205
  271.6 0.4 collective-permute-start.17
  272.0 1.7 collective-permute-start.21
  273.7 3.6 %collective-permute-done.13.peer = bf16[32,4096]{1,0:T(8,128)(2,1)S(1)} collective-permute-done((bf16[32,4096]{1,0:T(8,128)(2,1)S(1)}, bf16[32,4096]{1,0:T(8,128)(2,1)S(1)}, u32[]{:S(2)}, u32[]{:S(2)}) %collective-permute-start.13) | collective-permute-done | bytes 262176 | tf_op jit(solution)/shard_map/ppermute | solution.py:205
  277.3 0.4 collective-permute-start.25
  277.7 5.1 %collective-permute-done.17.peer = bf16[32,4096]{1,0:T(8,128)(2,1)S(1)} collective-permute-done((bf16[32,4096]{1,0:T(8,128)(2,1)S(1)}, bf16[32,4096]{1,0:T(8,128)(2,1)S(1)}, u32[]{:S(2)}, u32[]{:S(2)}) %collective-permute-start.17) | collective-permute-done | bytes 262176 | tf_op jit(solution)/shard_map/ppermute | solution.py:205
  282.9 0.4 collective-permute-start.29
  283.2 5.2 %collective-permute-done.21.peer = bf16[32,4096]{1,0:T(8,128)(2,1)S(1)} collective-permute-done((bf16[32,4096]{1,0:T(8,128)(2,1)S(1)}, bf16[32,4096]{1,0:T(8,128)(2,1)S(1)}, u32[]{:S(2)}, u32[]{:S(2)}) %collective-permute-start.21) | collective-permute-done | bytes 262176 | tf_op jit(solution)/shard_map/ppermute | solution.py:205
  288.5 0.5 collective-permute-start.15
  289.0 5.1 %collective-permute-done.25.peer = bf16[32,4096]{1,0:T(8,128)(2,1)S(1)} collective-permute-done((bf16[32,4096]{1,0:T(8,128)(2,1)S(1)}, bf16[32,4096]{1,0:T(8,128)(2,1)S(1)}, u32[]{:S(2)}, u32[]{:S(2)}) %collective-permute-start.25) | collective-permute-done | bytes 262176 | tf_op jit(solution)/shard_map/ppermute | solution.py:205
  294.1 4.9 %collective-permute-done.29.peer = bf16[32,4096]{1,0:T(8,128)(2,1)S(1)} collective-permute-done((bf16[32,4096]{1,0:T(8,128)(2,1)S(1)}, bf16[32,4096]{1,0:T(8,128)(2,1)S(1)}, u32[]{:S(2)}, u32[]{:S(2)}) %collective-permute-start.29) | collective-permute-done | bytes 262176 | tf_op jit(solution)/shard_map/ppermute | solution.py:205
  299.0 0.5 collective-permute-start.23
  299.5 0.5 collective-permute-start.11
  300.0 0.5 collective-permute-done.31.peer2
  300.5 0.1 collective-permute-start.7
  300.7 1.9 finish.8.rest_0_
  302.5 0.4 collective-permute-start.2
  302.9 0.1 collective-permute-start.3
  303.0 1.9 finish.9.rest_0_
  304.9 1.9 finish.10.rest_0_
  306.8 1.9 finish.11.rest_0_
  308.6 1.9 finish.12.rest_0_
  310.5 1.9 finish.13.rest_0_
  312.4 1.9 finish.14.rest_0_
  314.3 1.9 finish.15
  (64 shorter events, 0.8 us)
Async XLA Ops:
  0.7 9.4 %copy-start = (bf16[512,4096]{1,0:T(8,128)(2,1)S(1)}, bf16[512,4096]{1,0:T(8,128)(2,1)}, u32[]{:S(2)}) copy-start(bf16[512,4096]{1,0:T(8,128)(2,1)} %hid.15) | copy-start | bytes 12582916
  0.7 9.4 %copy-start.7 = (bf16[4096,1024]{1,0:T(8,128)(2,1)S(1)}, bf16[4096,1024]{1,0:T(8,128)(2,1)}, u32[]{:S(2)}) copy-start(bf16[4096,1024]{1,0:T(8,128)(2,1)} %param.12) | copy-start | bytes 25165828
  10.1 13.4 %copy-start.5 = (f32[1024]{0:T(1024)S(1)}, f32[1024]{0:T(1024)}, u32[]{:S(2)}) copy-start(f32[1024]{0:T(1024)} %param.17) | copy-start | bytes 12292
  14.7 9.6 %copy-start.4 = (s32[512]{0:T(512)S(1)}, s32[512]{0:T(512)}, u32[]{:S(2)}) copy-start(s32[512]{0:T(512)} %refs_0_.15) | copy-start | bytes 6148
  14.7 9.6 %copy-start.6 = (f32[1024]{0:T(1024)S(1)}, f32[1024]{0:T(1024)}, u32[]{:S(2)}) copy-start(f32[1024]{0:T(1024)} %param.16) | copy-start | bytes 12292
  23.5 3.4 %copy-start.8 = (bf16[4096,1024]{1,0:T(8,128)(2,1)S(1)}, bf16[4096,1024]{1,0:T(8,128)(2,1)}, u32[]{:S(2)}) copy-start(bf16[4096,1024]{1,0:T(8,128)(2,1)} %param.14) | copy-start | bytes 25165828
  24.3 4.0 %copy-start.1 = (bf16[512,4096]{1,0:T(8,128)(2,1)S(1)}, bf16[512,4096]{1,0:T(8,128)(2,1)}, u32[]{:S(2)}) copy-start(bf16[512,4096]{1,0:T(8,128)(2,1)} %hid.15) | copy-start | bytes 12582916
  34.0 3.0 slice-start
  34.0 3.5 %slice-start.1 = ((s8[8388608]{0:T(1024)(128)(4,1)}), s8[4194304]{0:T(1024)(128)(4,1)S(1)}, s32[]{:S(2)}) async-start(s8[8388608]{0:T(1024)(128)(4,1)} %bitcast.21), calls=%async_computation.1 | async-start | bytes 8388608
  248.5 52.2 %copy-start.2 = (bf16[512,4096]{1,0:T(8,128)(2,1)S(1)}, bf16[512,4096]{1,0:T(8,128)(2,1)}, u32[]{:S(2)}) copy-start(bf16[512,4096]{1,0:T(8,128)(2,1)} %hid.15) | copy-start | bytes 12582916
  248.5 52.1 %copy-start.3 = (f32[4096]{0:T(1024)S(1)}, f32[4096]{0:T(1024)}, u32[]{:S(2)}) copy-start(f32[4096]{0:T(1024)} %param.18) | copy-start | bytes 49156
  248.5 1.6 collective-permute-start
  248.6 1.9 collective-permute-start.4
  249.1 1.8 collective-permute-start.8
  249.1 2.1 collective-permute-start.12
  249.6 2.1 collective-permute-start.16
  250.1 1.9 collective-permute-start.20
  250.5 3.1 collective-permute-start.24
  250.8 3.3 %collective-permute-start.28 = (bf16[32,4096]{1,0:T(8,128)(2,1)S(1)}, bf16[32,4096]{1,0:T(8,128)(2,1)S(1)}, u32[]{:S(2)}, u32[]{:S(2)}) collective-permute-start(bf16[32,4096]{1,0:T(8,128)(2,1)S(1)} %get-tuple-element.64), channel_id=1, source_target_pairs={{0,1},{1,0},{2,3},{3,2},{4,5},{5,4},{6,7},{7,6}} | collective-permute-start | bytes 786440 | tf_op jit(solution)/shard_map/ppermute | solution.py:203
  251.2 20.8 %collective-permute-start.9 = (bf16[32,4096]{1,0:T(8,128)(2,1)S(1)}, bf16[32,4096]{1,0:T(8,128)(2,1)S(1)}, u32[]{:S(2)}, u32[]{:S(2)}) collective-permute-start(bf16[32,4096]{1,0:T(8,128)(2,1)S(1)} %add_convert_fusion.7.own), channel_id=1, source_target_pairs={{0,2},{2,0},{1,3},{3,1},{4,6},{6,4},{5,7},{7,5}} | collective-permute-start | bytes 786440 | tf_op jit(solution)/shard_map/ppermute | solution.py:205
  251.7 20.3 %collective-permute-start.10 = (bf16[32,4096]{1,0:T(8,128)(2,1)S(1)}, bf16[32,4096]{1,0:T(8,128)(2,1)S(1)}, u32[]{:S(2)}, u32[]{:S(2)}) collective-permute-start(bf16[32,4096]{1,0:T(8,128)(2,1)S(1)} %add_convert_fusion.7.own), channel_id=1, source_target_pairs={{0,1},{1,0},{2,3},{3,2},{4,5},{5,4},{6,7},{7,6}} | collective-permute-start | bytes 786440 | tf_op jit(solution)/shard_map/ppermute | solution.py:206
  252.0 14.0 %collective-permute-start.1 = (bf16[32,4096]{1,0:T(8,128)(2,1)S(1)}, bf16[32,4096]{1,0:T(8,128)(2,1)S(1)}, u32[]{:S(2)}, u32[]{:S(2)}) collective-permute-start(bf16[32,4096]{1,0:T(8,128)(2,1)S(1)} %add_convert_fusion.9.own), channel_id=1, source_target_pairs={{0,2},{2,0},{1,3},{3,1},{4,6},{6,4},{5,7},{7,5}} | collective-permute-start | bytes 786440 | tf_op jit(solution)/shard_map/ppermute | solution.py:205
  253.5 18.1 %collective-permute-start.5 = (bf16[32,4096]{1,0:T(8,128)(2,1)S(1)}, bf16[32,4096]{1,0:T(8,128)(2,1)S(1)}, u32[]{:S(2)}, u32[]{:S(2)}) collective-permute-start(bf16[32,4096]{1,0:T(8,128)(2,1)S(1)} %add_convert_fusion.8.own), channel_id=1, source_target_pairs={{0,2},{2,0},{1,3},{3,1},{4,6},{6,4},{5,7},{7,5}} | collective-permute-start | bytes 786440 | tf_op jit(solution)/shard_map/ppermute | solution.py:205
  254.1 23.2 %collective-permute-start.13 = (bf16[32,4096]{1,0:T(8,128)(2,1)S(1)}, bf16[32,4096]{1,0:T(8,128)(2,1)S(1)}, u32[]{:S(2)}, u32[]{:S(2)}) collective-permute-start(bf16[32,4096]{1,0:T(8,128)(2,1)S(1)} %add_convert_fusion.6.own), channel_id=1, source_target_pairs={{0,2},{2,0},{1,3},{3,1},{4,6},{6,4},{5,7},{7,5}} | collective-permute-start | bytes 786440 | tf_op jit(solution)/shard_map/ppermute | solution.py:205
  266.0 11.3 %collective-permute-start.14 = (bf16[32,4096]{1,0:T(8,128)(2,1)S(1)}, bf16[32,4096]{1,0:T(8,128)(2,1)S(1)}, u32[]{:S(2)}, u32[]{:S(2)}) collective-permute-start(bf16[32,4096]{1,0:T(8,128)(2,1)S(1)} %add_convert_fusion.6.own), channel_id=1, source_target_pairs={{0,1},{1,0},{2,3},{3,2},{4,5},{5,4},{6,7},{7,6}} | collective-permute-start | bytes 786440 | tf_op jit(solution)/shard_map/ppermute | solution.py:206
  271.6 11.2 %collective-permute-start.17 = (bf16[32,4096]{1,0:T(8,128)(2,1)S(1)}, bf16[32,4096]{1,0:T(8,128)(2,1)S(1)}, u32[]{:S(2)}, u32[]{:S(2)}) collective-permute-start(bf16[32,4096]{1,0:T(8,128)(2,1)S(1)} %add_convert_fusion.5.own), channel_id=1, source_target_pairs={{0,2},{2,0},{1,3},{3,1},{4,6},{6,4},{5,7},{7,5}} | collective-permute-start | bytes 786440 | tf_op jit(solution)/shard_map/ppermute | solution.py:205
  272.0 11.2 %collective-permute-start.18 = (bf16[32,4096]{1,0:T(8,128)(2,1)S(1)}, bf16[32,4096]{1,0:T(8,128)(2,1)S(1)}, u32[]{:S(2)}, u32[]{:S(2)}) collective-permute-start(bf16[32,4096]{1,0:T(8,128)(2,1)S(1)} %add_convert_fusion.5.own), channel_id=1, source_target_pairs={{0,1},{1,0},{2,3},{3,2},{4,5},{5,4},{6,7},{7,6}} | collective-permute-start | bytes 786440 | tf_op jit(solution)/shard_map/ppermute | solution.py:206
  272.0 16.5 %collective-permute-start.21 = (bf16[32,4096]{1,0:T(8,128)(2,1)S(1)}, bf16[32,4096]{1,0:T(8,128)(2,1)S(1)}, u32[]{:S(2)}, u32[]{:S(2)}) collective-permute-start(bf16[32,4096]{1,0:T(8,128)(2,1)S(1)} %add_convert_fusion.4.own), channel_id=1, source_target_pairs={{0,2},{2,0},{1,3},{3,1},{4,6},{6,4},{5,7},{7,5}} | collective-permute-start | bytes 786440 | tf_op jit(solution)/shard_map/ppermute | solution.py:205
  277.2 11.2 %collective-permute-start.22 = (bf16[32,4096]{1,0:T(8,128)(2,1)S(1)}, bf16[32,4096]{1,0:T(8,128)(2,1)S(1)}, u32[]{:S(2)}, u32[]{:S(2)}) collective-permute-start(bf16[32,4096]{1,0:T(8,128)(2,1)S(1)} %add_convert_fusion.4.own), channel_id=1, source_target_pairs={{0,1},{1,0},{2,3},{3,2},{4,5},{5,4},{6,7},{7,6}} | collective-permute-start | bytes 786440 | tf_op jit(solution)/shard_map/ppermute | solution.py:206
  277.3 16.8 %collective-permute-start.25 = (bf16[32,4096]{1,0:T(8,128)(2,1)S(1)}, bf16[32,4096]{1,0:T(8,128)(2,1)S(1)}, u32[]{:S(2)}, u32[]{:S(2)}) collective-permute-start(bf16[32,4096]{1,0:T(8,128)(2,1)S(1)} %add_convert_fusion.3.own), channel_id=1, source_target_pairs={{0,2},{2,0},{1,3},{3,1},{4,6},{6,4},{5,7},{7,5}} | collective-permute-start | bytes 786440 | tf_op jit(solution)/shard_map/ppermute | solution.py:205
  282.9 16.1 %collective-permute-start.29 = (bf16[32,4096]{1,0:T(8,128)(2,1)S(1)}, bf16[32,4096]{1,0:T(8,128)(2,1)S(1)}, u32[]{:S(2)}, u32[]{:S(2)}) collective-permute-start(bf16[32,4096]{1,0:T(8,128)(2,1)S(1)} %add_convert_fusion.2.own), channel_id=1, source_target_pairs={{0,2},{2,0},{1,3},{3,1},{4,6},{6,4},{5,7},{7,5}} | collective-permute-start | bytes 786440 | tf_op jit(solution)/shard_map/ppermute | solution.py:205
  283.2 15.8 %collective-permute-start.26 = (bf16[32,4096]{1,0:T(8,128)(2,1)S(1)}, bf16[32,4096]{1,0:T(8,128)(2,1)S(1)}, u32[]{:S(2)}, u32[]{:S(2)}) collective-permute-start(bf16[32,4096]{1,0:T(8,128)(2,1)S(1)} %add_convert_fusion.3.own), channel_id=1, source_target_pairs={{0,1},{1,0},{2,3},{3,2},{4,5},{5,4},{6,7},{7,6}} | collective-permute-start | bytes 786440 | tf_op jit(solution)/shard_map/ppermute | solution.py:206
  288.5 11.0 %collective-permute-start.30 = (bf16[32,4096]{1,0:T(8,128)(2,1)S(1)}, bf16[32,4096]{1,0:T(8,128)(2,1)S(1)}, u32[]{:S(2)}, u32[]{:S(2)}) collective-permute-start(bf16[32,4096]{1,0:T(8,128)(2,1)S(1)} %add_convert_fusion.2.own), channel_id=1, source_target_pairs={{0,1},{1,0},{2,3},{3,2},{4,5},{5,4},{6,7},{7,6}} | collective-permute-start | bytes 786440 | tf_op jit(solution)/shard_map/ppermute | solution.py:206
  288.5 11.0 %collective-permute-start.15 = (bf16[32,4096]{1,0:T(8,128)(2,1)S(1)}, bf16[32,4096]{1,0:T(8,128)(2,1)S(1)}, u32[]{:S(2)}, u32[]{:S(2)}) collective-permute-start(bf16[32,4096]{1,0:T(8,128)(2,1)S(1)} %collective-permute-done.13.peer), channel_id=1, source_target_pairs={{0,1},{1,0},{2,3},{3,2},{4,5},{5,4},{6,7},{7,6}} | collective-permute-start | bytes 786440 | tf_op jit(solution)/shard_map/ppermute | solution.py:207
  294.1 5.9 %collective-permute-start.19 = (bf16[32,4096]{1,0:T(8,128)(2,1)S(1)}, bf16[32,4096]{1,0:T(8,128)(2,1)S(1)}, u32[]{:S(2)}, u32[]{:S(2)}) collective-permute-start(bf16[32,4096]{1,0:T(8,128)(2,1)S(1)} %collective-permute-done.17.peer), channel_id=1, source_target_pairs={{0,1},{1,0},{2,3},{3,2},{4,5},{5,4},{6,7},{7,6}} | collective-permute-start | bytes 786440 | tf_op jit(solution)/shard_map/ppermute | solution.py:207
  299.0 1.5 collective-permute-start.31
  299.0 3.5 %collective-permute-start.23 = (bf16[32,4096]{1,0:T(8,128)(2,1)S(1)}, bf16[32,4096]{1,0:T(8,128)(2,1)S(1)}, u32[]{:S(2)}, u32[]{:S(2)}) collective-permute-start(bf16[32,4096]{1,0:T(8,128)(2,1)S(1)} %collective-permute-done.21.peer), channel_id=1, source_target_pairs={{0,1},{1,0},{2,3},{3,2},{4,5},{5,4},{6,7},{7,6}} | collective-permute-start | bytes 786440 | tf_op jit(solution)/shard_map/ppermute | solution.py:207
  299.5 3.4 %collective-permute-start.27 = (bf16[32,4096]{1,0:T(8,128)(2,1)S(1)}, bf16[32,4096]{1,0:T(8,128)(2,1)S(1)}, u32[]{:S(2)}, u32[]{:S(2)}) collective-permute-start(bf16[32,4096]{1,0:T(8,128)(2,1)S(1)} %collective-permute-done.25.peer), channel_id=1, source_target_pairs={{0,1},{1,0},{2,3},{3,2},{4,5},{5,4},{6,7},{7,6}} | collective-permute-start | bytes 786440 | tf_op jit(solution)/shard_map/ppermute | solution.py:207
  299.5 11.0 %collective-permute-start.11 = (bf16[32,4096]{1,0:T(8,128)(2,1)S(1)}, bf16[32,4096]{1,0:T(8,128)(2,1)S(1)}, u32[]{:S(2)}, u32[]{:S(2)}) collective-permute-start(bf16[32,4096]{1,0:T(8,128)(2,1)S(1)} %collective-permute-done.9.peer), channel_id=1, source_target_pairs={{0,1},{1,0},{2,3},{3,2},{4,5},{5,4},{6,7},{7,6}} | collective-permute-start | bytes 786440 | tf_op jit(solution)/shard_map/ppermute | solution.py:207
  300.0 12.4 %collective-permute-start.6 = (bf16[32,4096]{1,0:T(8,128)(2,1)S(1)}, bf16[32,4096]{1,0:T(8,128)(2,1)S(1)}, u32[]{:S(2)}, u32[]{:S(2)}) collective-permute-start(bf16[32,4096]{1,0:T(8,128)(2,1)S(1)} %add_convert_fusion.8.own), channel_id=1, source_target_pairs={{0,1},{1,0},{2,3},{3,2},{4,5},{5,4},{6,7},{7,6}} | collective-permute-start | bytes 786440 | tf_op jit(solution)/shard_map/ppermute | solution.py:206
  300.5 11.9 %collective-permute-start.7 = (bf16[32,4096]{1,0:T(8,128)(2,1)S(1)}, bf16[32,4096]{1,0:T(8,128)(2,1)S(1)}, u32[]{:S(2)}, u32[]{:S(2)}) collective-permute-start(bf16[32,4096]{1,0:T(8,128)(2,1)S(1)} %collective-permute-done.5.peer), channel_id=1, source_target_pairs={{0,1},{1,0},{2,3},{3,2},{4,5},{5,4},{6,7},{7,6}} | collective-permute-start | bytes 786440 | tf_op jit(solution)/shard_map/ppermute | solution.py:207
  302.5 11.8 %collective-permute-start.2 = (bf16[32,4096]{1,0:T(8,128)(2,1)S(1)}, bf16[32,4096]{1,0:T(8,128)(2,1)S(1)}, u32[]{:S(2)}, u32[]{:S(2)}) collective-permute-start(bf16[32,4096]{1,0:T(8,128)(2,1)S(1)} %add_convert_fusion.9.own), channel_id=1, source_target_pairs={{0,1},{1,0},{2,3},{3,2},{4,5},{5,4},{6,7},{7,6}} | collective-permute-start | bytes 786440 | tf_op jit(solution)/shard_map/ppermute | solution.py:206
  302.9 11.4 %collective-permute-start.3 = (bf16[32,4096]{1,0:T(8,128)(2,1)S(1)}, bf16[32,4096]{1,0:T(8,128)(2,1)S(1)}, u32[]{:S(2)}, u32[]{:S(2)}) collective-permute-start(bf16[32,4096]{1,0:T(8,128)(2,1)S(1)} %collective-permute-done.1.peer), channel_id=1, source_target_pairs={{0,1},{1,0},{2,3},{3,2},{4,5},{5,4},{6,7},{7,6}} | collective-permute-start | bytes 786440 | tf_op jit(solution)/shard_map/ppermute | solution.py:207

commit v2 on v1

v2 whole, which is shorter than its diff:
```python
import functools

import jax
import jax.numpy as jnp
from jax import lax
from jax.experimental import pallas as pl
from jax.experimental.pallas import tpu as pltpu
from jax.sharding import PartitionSpec as P


NORM_EPS = 1e-6
ROPE_BASE = 500000.0
CHUNKS = (160, 128, 128, 96)
BLOCK = 8
DEPTH = 10
FINAL_ROWS = 16
PARTNER = [(0, 1), (1, 0), (2, 3), (3, 2)]
PEER = [(0, 2), (2, 0), (1, 3), (3, 1)]

VMEM = pl.BlockSpec(memory_space=pltpu.VMEM)
SMEM = pl.BlockSpec(memory_space=pltpu.SMEM)
ANY = pl.BlockSpec(memory_space=pl.ANY)


def attend_kernel(row0, rows, *refs):
    pos, core, q, kn, vn, wo, kc, vc = refs[:8]
    ko, vo, parts, kbuf, vbuf, o_f32, o_bf, isem, osem = refs[-9:]
    blocks = rows // BLOCK
    depth = kbuf.shape[0]
    ahead = depth - 3
    heads, dim = q.shape[1], q.shape[2]
    slots = kc.shape[1]
    span = slots * heads

    def copies_in(j, s):
        at = pl.ds(row0 + j * BLOCK, BLOCK)
        return (pltpu.make_async_copy(kc.at[at], kbuf.at[s], isem.at[s, 0]),
                pltpu.make_async_copy(vc.at[at], vbuf.at[s], isem.at[s, 1]))

    def copies_out(j, s):
        at = pl.ds(row0 + j * BLOCK, BLOCK)
        return (pltpu.make_async_copy(kbuf.at[s], ko.at[at], osem.at[s, 0]),
                pltpu.make_async_copy(vbuf.at[s], vo.at[at], osem.at[s, 1]))

    for j in range(min(ahead, blocks)):
        for c in copies_in(j, j):
            c.start()

    lane = lax.broadcasted_iota(jnp.int32, (heads, span), 1)
    head = lax.broadcasted_iota(jnp.int32, (heads, span), 0)
    slot_of = jnp.where(lax.rem(lane, heads) == head, lax.div(lane, heads), slots)

    def arrive(i):
        s = lax.rem(i, depth)
        for c in copies_in(i, s):
            c.wait()
        for r in range(BLOCK):
            row = row0 + i * BLOCK + r
            p = pos[row]
            kbuf[s, r, p] = kn[row]
            vbuf[s, r, p] = vn[row]

    def scores(i):
        s = lax.rem(i, depth)
        out = []
        for r in range(BLOCK):
            row = row0 + i * BLOCK + r
            k = kbuf[s, r].reshape(span, dim)
            score = lax.dot_general(q[row], k, (((1,), (1,)), ((), ())), preferred_element_type=jnp.float32)
            out.append(jnp.where(slot_of <= pos[row], score * dim ** -0.5, -1e30))
        return jnp.concatenate(out, axis=0)

    def softmax(score):
        e = jnp.exp(score - jnp.max(score, axis=-1, keepdims=True))
        return (e / jnp.sum(e, axis=-1, keepdims=True)).astype(jnp.bfloat16)

    def mix(i, prob):
        s = lax.rem(i, depth)
        for r in range(BLOCK):
            v = vbuf[s, r].reshape(span, dim)
            at = pl.ds((i * BLOCK + r) * heads, heads)
            o_f32[at] = jnp.dot(prob[r * heads:(r + 1) * heads], v, preferred_element_type=jnp.float32)
        for c in copies_out(i, s):
            c.start()

    arrive(0)

    def step(i, score):
        nxt = i - 1 + ahead

        @pl.when(nxt < blocks)
        def _():
            @pl.when(nxt >= depth)
            def _():
                for c in copies_out(nxt - depth, lax.rem(nxt, depth)):
                    c.wait()

            for c in copies_in(nxt, lax.rem(nxt, depth)):
                c.start()

        arrive(i)
        prob = softmax(score)
        new = scores(i)
        mix(i - 1, prob)
        return new

    last = lax.fori_loop(1, blocks, step, scores(0))
    mix(blocks - 1, softmax(last))
    for h in range(heads):
        o_bf[:, h * dim:(h + 1) * dim] = o_f32[pl.ds(h, rows, stride=heads), :].astype(jnp.bfloat16)
    half = rows // 2
    for j, which in ((0, core[0]), (1, 1 - core[0])):
        o = o_bf[pl.ds(pl.multiple_of(which * half, 16), half), :]
        for n in range(0, wo.shape[1], 512):
            parts[j, :, n:n + 512] = jnp.dot(o, wo[:, n:n + 512], preferred_element_type=jnp.float32).astype(jnp.bfloat16)
    for j in range(max(0, blocks - depth), blocks):
        for c in copies_out(j, j % depth):
            c.wait()


def attend(row0, rows, pos, core, q, kn, vn, wo, kc, vc, prev):
    width = wo.shape[1]
    args = (pos, core, q, kn, vn, wo, kc, vc) + prev
    share = jax.ShapeDtypeStruct((2, rows // 2, width), jnp.bfloat16)
    return pl.pallas_call(
        functools.partial(attend_kernel, row0, rows),
        out_shape=(jax.ShapeDtypeStruct(kc.shape, kc.dtype), jax.ShapeDtypeStruct(vc.shape, vc.dtype), share),
        in_specs=[SMEM, SMEM, VMEM, VMEM, VMEM, VMEM, ANY, ANY] + [ANY] * len(prev),
        out_specs=(ANY, ANY, VMEM),
        input_output_aliases={8: 0, 9: 1} if prev else {},
        scratch_shapes=[
            pltpu.VMEM((DEPTH, BLOCK) + kc.shape[1:], kc.dtype),
            pltpu.VMEM((DEPTH, BLOCK) + vc.shape[1:], vc.dtype),
            pltpu.VMEM((rows * q.shape[1], q.shape[2]), jnp.float32),
            pltpu.VMEM((rows, q.shape[1] * q.shape[2]), jnp.bfloat16),
            pltpu.SemaphoreType.DMA((DEPTH, 2)),
            pltpu.SemaphoreType.DMA((DEPTH, 2)),
        ],
        compiler_params=pltpu.CompilerParams(vmem_limit_bytes=32 * 2 ** 20),
        cost_estimate=pl.CostEstimate(flops=rows * 75_000_000, bytes_accessed=rows * 4 * 65536, transcendentals=0),
        name='attend',
    )(*args)


def final_kernel(core, hid, own, peer, mine, got, peer2, gain, *rest):
    out = rest[-1]
    j = pl.program_id(0)

    def emit(a, b):
        total = a + b[...].astype(jnp.float32)
        inv = lax.rsqrt(jnp.mean(total * total, axis=-1, keepdims=True) + NORM_EPS)
        out[...] = (hid[...].astype(jnp.float32) + total * inv * gain[...]).astype(jnp.bfloat16)

    @pl.when(j == 0)
    def _():
        emit(own[...].astype(jnp.float32), peer)

    @pl.when(j == 1)
    def _():
        chip = (mine[...].astype(jnp.float32) + got[...].astype(jnp.float32)).astype(jnp.bfloat16)
        emit(chip.astype(jnp.float32), peer2)


def finish(row0, rows, core, hidden, own, peer, parts, got, peer2, gain, prev):
    width = hidden.shape[1]
    blocks = rows // 2 // FINAL_ROWS
    first = row0 // FINAL_ROWS

    def place(j, b, core):
        which = core[0] + j - 2 * core[0] * j
        return (first + which * blocks + b, 0)

    def early(j, b, core):
        return (b + j * (blocks - 1 - b), 0)

    def late(j, b, core):
        return (b * j, 0)

    block = (FINAL_ROWS, width)
    return pl.pallas_call(
        final_kernel,
        out_shape=jax.ShapeDtypeStruct(hidden.shape, hidden.dtype),
        grid_spec=pltpu.PrefetchScalarGridSpec(
            num_scalar_prefetch=1,
            grid=(2, blocks),
            in_specs=[
                pl.BlockSpec(block, place), pl.BlockSpec(block, early), pl.BlockSpec(block, early),
                pl.BlockSpec((None,) + block, lambda j, b, core: (1,) + late(j, b, core)),
                pl.BlockSpec((None,) + block, lambda j, b, core: (0,) + late(j, b, core)),
                pl.BlockSpec(block, late), pl.BlockSpec((1, width), lambda j, b, core: (0, 0)),
            ] + [ANY] * len(prev),
            out_specs=pl.BlockSpec(block, place),
        ),
        input_output_aliases={8: 0} if prev else {},
        compiler_params=pltpu.CompilerParams(vmem_limit_bytes=8 * 2 ** 20),
        cost_estimate=pl.CostEstimate(flops=rows * 8_000_000, bytes_accessed=rows * 32768, transcendentals=0),
        name='finish',
    )(core, hidden, own, peer, parts, got, peer2, gain, *prev)


def apply_rope(heads_val, positions):
    head_dim = heads_val.shape[-1]
    half = head_dim // 2
    inv_freq = ROPE_BASE ** (-2.0 * jnp.arange(half, dtype=jnp.float32) / head_dim)
    angles = positions.astype(jnp.float32)[:, None, None] * inv_freq[None, None, :]
    cos_tab = jnp.cos(angles)
    sin_tab = jnp.sin(angles)
    wide = heads_val.astype(jnp.float32)
    first = wide[..., :half]
    second = wide[..., half:]
    return jnp.concatenate([first * cos_tab - second * sin_tab, second * cos_tab + first * sin_tab], axis=-1).astype(jnp.bfloat16)


def solution(mesh):
    def local_step(hidden, w_q, w_k, w_v, w_o, q_norm_w, k_norm_w, post_norm_w, k_cache, v_cache, positions):
        n_rows, width = hidden.shape
        local_heads, head_dim = k_cache.shape[2], k_cache.shape[3]
        q_local = jnp.dot(hidden, w_q, preferred_element_type=jnp.float32).astype(jnp.bfloat16).astype(jnp.float32)
        k_local = jnp.dot(hidden, w_k, preferred_element_type=jnp.float32).astype(jnp.bfloat16).astype(jnp.float32)
        v_local = jnp.dot(hidden, w_v, preferred_element_type=jnp.float32).astype(jnp.bfloat16)
        energy = jnp.stack([jnp.sum(q_local * q_local, axis=-1), jnp.sum(k_local * k_local, axis=-1)])
        energy = lax.psum(energy, 'tp')
        inv_rms = lax.rsqrt(energy / width + NORM_EPS)
        q_normed = (q_local * inv_rms[0][:, None] * q_norm_w).astype(jnp.bfloat16).reshape(n_rows, local_heads, head_dim)
        k_normed = (k_local * inv_rms[1][:, None] * k_norm_w).astype(jnp.bfloat16).reshape(n_rows, local_heads, head_dim)
        q_rot = apply_rope(q_normed, positions)
        k_rot = apply_rope(k_normed, positions)
        v_new = v_local.reshape(n_rows, local_heads, head_dim)
        core = jnp.reshape(lax.rem(lax.axis_index('tp'), 2), (1,)).astype(jnp.int32)
        gain = post_norm_w.reshape(1, width)

        caches, out, row0 = (), (), 0
        for rows in CHUNKS:
            k_out, v_out, parts = attend(row0, rows, positions, core, q_rot, k_rot, v_new, w_o, k_cache, v_cache, caches)
            caches = (k_out, v_out)
            got = lax.ppermute(parts, 'tp', PARTNER)
            own = (parts[0].astype(jnp.float32) + got[1].astype(jnp.float32)).astype(jnp.bfloat16)
            peer = lax.ppermute(own, 'tp', PEER)
            peer2 = lax.ppermute(peer, 'tp', PARTNER)
            out = (finish(row0, rows, core, hidden, own, peer, parts, got, peer2, gain, out),)
            row0 += rows
        return out[0], caches[0], caches[1]

    cache_spec = P('dp', None, 'tp', None)
    return jax.shard_map(local_step, mesh=mesh, in_specs=(P('dp', None), P(None, 'tp'), P(None, 'tp'), P(None, 'tp'), P('tp', None), P('tp'), P('tp'), P(None), cache_spec, cache_spec, P('dp')), out_specs=(P('dp', None), cache_spec, cache_spec), check_vma=False)
```

time: 316 us -> 160 us (0.51)
  Pallas kernels: 226 us -> 76.6 us
  starting transfers between devices: 10.7 us -> 4.41 us
  local copies, waits for them, and re-layouts: 4.99 us -> 1.48 us
    pallas_call x8 -> x4, Pallas kernels: 211 us -> 62.1 us  [attend(): pl.pallas_call(functools.partial(attend_kernel, row0, rows), out_shape=(j...]
    dot_general x1, matrix products: 4.5 us -> 9.28 us  [local_step(): jnp.dot(hidden, w_v, preferred_element_type=jnp.float32)]
    dot_general x1, matrix products: 9.36 us -> 4.61 us  [local_step(): jnp.dot(hidden, w_k, preferred_element_type=jnp.float32)]
    ppermute x8 -> x4, starting transfers between devices: 6.7 us -> 2.84 us  [local_step(): peer = lax.ppermute(own, 'tp', PEER)]
    unnamed x25, local copies, waits for them, and re-layouts: 4.99 us -> 1.47 us
    ppermute x8 -> x4, waiting for transfers between devices: 39.9 us -> 43 us  [local_step(): peer = lax.ppermute(own, 'tp', PEER)]
    pallas_call x8 -> x4, Pallas kernels: 15 us -> 14.5 us  [finish(): pl.pallas_call(final_kernel, out_shape=jax.ShapeDtypeStruct(hidden.shape,...]
  transfers between devices with their start and end apart: 32 -> 12, of which waited for: 13 -> 4; matrix products, arithmetic and copies ran while one was open for 0% -> 0% of each run, Pallas kernels for 4% -> 15%
where the time goes in v2:
time: 160 us
  Pallas kernels  76.6 us (48%)
  waiting for transfers between devices  43.9 us (27%)
  matrix products  18.5 us (12%)
  blocking collectives  8.72 us (5%)
  other arithmetic  5.42 us (3%)
  starting transfers between devices  4.41 us (3%)
    pallas_call x4, Pallas kernels, attend(): pl.pallas_call(functools.partial(attend_kernel, row0, rows), out_shape=(j...  62.1 us
    ppermute x4, waiting for transfers between devices, local_step(): peer = lax.ppermute(own, 'tp', PEER)  43 us
    pallas_call x4, Pallas kernels, finish(): pl.pallas_call(final_kernel, out_shape=jax.ShapeDtypeStruct(hidden.shape,...  14.5 us
    dot_general x1, matrix products, local_step(): jnp.dot(hidden, w_v, preferred_element_type=jnp.float32)  9.28 us
    psum x1, blocking collectives, local_step(): energy = lax.psum(energy, 'tp')  8.72 us
    dot_general x1, matrix products, local_step(): jnp.dot(hidden, w_q, preferred_element_type=jnp.float32)  4.61 us
    dot_general x1, matrix products, local_step(): jnp.dot(hidden, w_k, preferred_element_type=jnp.float32)  4.61 us
  transfers between devices with their start and end apart: 12, of which 4 were waited for; matrix products, arithmetic and copies ran while one was open for 0% of the time, Pallas kernels for 15%

profile of v2, /device:TPU:0, one launch (start us, length us, event | category | flops | bytes accessed | tf_op | source)
XLA Modules:
  0.0 159.9 jit_solution(15741695222708747110)
XLA Ops:
  0.7 0.7 convert_element_type.98
  1.3 9.3 %fusion.6 = bf16[64,8,8,128]{3,1,2,0:T(8,128)(2,1)S(1)} fusion(bf16[512,4096]{1,0:T(8,128)(2,1)} %hid.7, bf16[4096,1024]{1,0:T(8,128)(2,1)} %param.14), kind=kOutput, calls=%fused_computation.19 | convolution fusion | flops 4295491584 | bytes 13631488 | tf_op jit(solution)/shard_map/dot_general | solution.py:220
  10.6 0.0 slice-start.2
  10.6 0.3 copy.25
  10.9 0.0 copy-done
  10.9 0.0 copy-done.6
  10.9 0.0 slice-start.3
  10.9 4.6 %fusion = (f32[512]{0:T(512)S(1)}, bf16[512,1024]{1,0:T(8,128)(2,1)S(1)}) fusion(bf16[512,4096]{1,0:T(8,128)(2,1)S(1)} %copy-done, bf16[4096,1024]{1,0:T(8,128)(2,1)S(1)} %copy-done.6), kind=kOutput, calls=%fused_computation.4 | convolution fusion | flops 4297063936 | bytes 13633536 | tf_op jit(solution)/shard_map/dot_general | solution.py:218
  15.6 0.0 slice-done.2
  15.6 0.0 slice-done.3
  15.6 0.0 copy-start.4
  15.6 4.6 %fusion.3 = (f32[512]{0:T(512)S(1)}, bf16[512,1024]{1,0:T(8,128)(2,1)S(1)}) fusion(bf16[512,4096]{1,0:T(8,128)(2,1)S(1)} %copy-done, bf16[4096,1024]{1,0:T(8,128)(2,1)S(1)} %bitcast.46), kind=kOutput, calls=%fused_computation.7 | convolution fusion | flops 4297063936 | bytes 13633536 | tf_op jit(solution)/shard_map/dot_general | solution.py:219
  20.2 8.7 %psum.7 = f32[2,512]{1,0:T(2,128)S(1)} all-reduce(f32[2,512]{1,0:T(2,128)S(1)} %pad_maximum_fusion.2), channel_id=1, replica_groups=mesh['dp'=2,'tp'=4] {'tp'}, use_global_device_ids=true, to_apply=%region_2.0 | all-reduce | flops 1024 | bytes 8192 | tf_op jit(solution)/shard_map/psum | solution.py:222
  29.0 0.3 convert_bitcast_fusion.1
  29.2 0.0 copy-start.5
  29.3 0.5 copy.23
  29.7 0.2 copy-done.5
  29.9 0.3 convert_bitcast_fusion
  30.2 0.0 slice-start
  30.2 0.5 copy.24
  30.7 1.0 multiply_cosine_fusion
  31.7 0.0 slice-start.1
  31.7 1.5 subtract_convert_fusion
  33.2 0.0 copy-start.3
  33.3 1.2 pad_maximum_fusion
  34.5 17.8 %attend.4 = (bf16[512,32,8,128]{3,2,1,0:T(8,128)(2,1)}, bf16[512,32,8,128]{3,2,1,0:T(8,128)(2,1)}, bf16[2,80,4096]{2,1,0:T(8,128)(2,1)S(1)}) custom-call(s32[512]{0:T(512)S(1)} %copy-done.3, s32[1]{0:T(128)} %bitcast.refs_1_.core, bf16[512,8,128]{2,1,0:T(8,128)(2,1)S(1)} %get-tuple-element.41.refs_2_, bf16[512,8,128]{2,1,0:T(8,128)(2,1)S(1)} %get-tuple-element.42.refs_3_, ...), custom_call_target="tpu_custom_call" | custom-call | flops 12000000000 | bytes 41943040 | tf_op jit(solution)/shard_map/attend/pallas_call | solution.py:125
  52.2 15.8 %attend.5 = (bf16[512,32,8,128]{3,2,1,0:T(8,128)(2,1)}, bf16[512,32,8,128]{3,2,1,0:T(8,128)(2,1)}, bf16[2,64,4096]{2,1,0:T(8,128)(2,1)S(1)}) custom-call(s32[512]{0:T(512)S(1)} %copy-done.3, s32[1]{0:T(128)} %bitcast.refs_1_.core, bf16[512,8,128]{2,1,0:T(8,128)(2,1)S(1)} %get-tuple-element.41.refs_2_, ...), custom_call_target="tpu_custom_call", output_to_operand_aliasing={{0}: (8, {}), {1}: (9, {})} | custom-call | flops 9600000000 | bytes 33554432 | tf_op jit(solution)/shard_map/attend/pallas_call | solution.py:125
  68.1 15.8 %attend.6 = (bf16[512,32,8,128]{3,2,1,0:T(8,128)(2,1)}, bf16[512,32,8,128]{3,2,1,0:T(8,128)(2,1)}, bf16[2,64,4096]{2,1,0:T(8,128)(2,1)S(1)}) custom-call(s32[512]{0:T(512)S(1)} %copy-done.3, s32[1]{0:T(128)} %bitcast.refs_1_.core, bf16[512,8,128]{2,1,0:T(8,128)(2,1)S(1)} %get-tuple-element.41.refs_2_, ...), custom_call_target="tpu_custom_call", output_to_operand_aliasing={{0}: (8, {}), {1}: (9, {})} | custom-call | flops 9600000000 | bytes 33554432 | tf_op jit(solution)/shard_map/attend/pallas_call | solution.py:125
  83.9 0.0 collective-permute-start.3
  84.0 0.5 collective-permute-start.9
  84.5 12.7 %attend.7 = (bf16[512,32,8,128]{3,2,1,0:T(8,128)(2,1)}, bf16[512,32,8,128]{3,2,1,0:T(8,128)(2,1)}, bf16[2,48,4096]{2,1,0:T(8,128)(2,1)S(1)}) custom-call(s32[512]{0:T(512)S(1)} %copy-done.3, s32[1]{0:T(128)} %bitcast.refs_1_.core, bf16[512,8,128]{2,1,0:T(8,128)(2,1)S(1)} %get-tuple-element.41.refs_2_, ...), custom_call_target="tpu_custom_call", output_to_operand_aliasing={{0}: (8, {}), {1}: (9, {})} | custom-call | flops 7200000000 | bytes 25165824 | tf_op jit(solution)/shard_map/attend/pallas_call | solution.py:125
  97.1 0.1 collective-permute-start
  97.2 0.5 collective-permute-start.6
  97.7 0.0 collective-permute-done.3.got
  97.7 0.1 fusion.8.own
  97.8 0.0 copy-start.1
  97.8 0.0 copy-start.2
  97.8 0.4 collective-permute-start.4
  98.2 0.0 collective-permute-done.9.got
  98.2 0.2 fusion.7.own
  98.4 1.7 %collective-permute-start.10 = (bf16[80,4096]{1,0:T(8,128)(2,1)S(1)}, bf16[80,4096]{1,0:T(8,128)(2,1)S(1)}, u32[]{:S(2)}, u32[]{:S(2)}) collective-permute-start(bf16[80,4096]{1,0:T(8,128)(2,1)S(1)} %fusion.7.own), channel_id=1, source_target_pairs={{0,2},{2,0},{1,3},{3,1},{4,6},{6,4},{5,7},{7,5}} | collective-permute-start | bytes 1966088 | tf_op jit(solution)/shard_map/ppermute | solution.py:238
  100.0 0.9 collective-permute-done.6.got
  100.9 0.1 fusion.9.own
  101.1 0.4 collective-permute-start.7
  101.4 25.2 %collective-permute-done.10.peer = bf16[80,4096]{1,0:T(8,128)(2,1)S(1)} collective-permute-done((bf16[80,4096]{1,0:T(8,128)(2,1)S(1)}, bf16[80,4096]{1,0:T(8,128)(2,1)S(1)}, u32[]{:S(2)}, u32[]{:S(2)}) %collective-permute-start.10) | collective-permute-done | bytes 655392 | tf_op jit(solution)/shard_map/ppermute | solution.py:238
  126.7 0.0 collective-permute-start.11
  126.7 0.0 collective-permute-done.got
  126.7 0.1 fusion.10.own
  126.8 0.4 collective-permute-start.1
  127.2 10.7 %collective-permute-done.7.peer = bf16[64,4096]{1,0:T(8,128)(2,1)S(1)} collective-permute-done((bf16[64,4096]{1,0:T(8,128)(2,1)S(1)}, bf16[64,4096]{1,0:T(8,128)(2,1)S(1)}, u32[]{:S(2)}, u32[]{:S(2)}) %collective-permute-start.7) | collective-permute-done | bytes 524320 | tf_op jit(solution)/shard_map/ppermute | solution.py:238
  137.9 0.0 collective-permute-start.8
  137.9 0.0 collective-permute-done.4.peer
  137.9 0.5 collective-permute-start.5
  138.4 7.0 %collective-permute-done.1.peer = bf16[48,4096]{1,0:T(8,128)(2,1)S(1)} collective-permute-done((bf16[48,4096]{1,0:T(8,128)(2,1)S(1)}, bf16[48,4096]{1,0:T(8,128)(2,1)S(1)}, u32[]{:S(2)}, u32[]{:S(2)}) %collective-permute-start.1) | collective-permute-done | bytes 393248 | tf_op jit(solution)/shard_map/ppermute | solution.py:238
  145.4 0.0 collective-permute-start.2
  145.4 0.0 collective-permute-done.11.peer2
  145.4 0.0 copy-done.2
  145.4 4.5 %finish.4.rest_0_ = bf16[512,4096]{1,0:T(8,128)(2,1)} custom-call(s32[1]{0:T(128)} %bitcast.refs_1_.core, bf16[512,4096]{1,0:T(8,128)(2,1)S(1)} %copy-done.1, bf16[80,4096]{1,0:T(8,128)(2,1)S(1)} %fusion.7.own, bf16[80,4096]{1,0:T(8,128)(2,1)S(1)} %collective-permute-done.10.peer, bf16[2,80,4096]{2,1,0:T(8,128)(2,1)S(1)} %get-tuple-element.24.mine, ...), custom_call_target="tpu_custom_call" | custom-call | flops 1280000000 | bytes 5242880 | tf_op jit(solution)/shard_map/finish/pallas_call | solution.py:180
  149.9 0.0 collective-permute-done.8.peer2
  149.9 3.6 %finish.5.rest_0_ = bf16[512,4096]{1,0:T(8,128)(2,1)} custom-call(s32[1]{0:T(128)} %bitcast.refs_1_.core, bf16[512,4096]{1,0:T(8,128)(2,1)S(1)} %copy-done.1, bf16[64,4096]{1,0:T(8,128)(2,1)S(1)} %fusion.9.own, bf16[64,4096]{1,0:T(8,128)(2,1)S(1)} %collective-permute-done.7.peer, ...), custom_call_target="tpu_custom_call", output_to_operand_aliasing={{}: (8, {})} | custom-call | flops 1024000000 | bytes 4194304 | tf_op jit(solution)/shard_map/finish/pallas_call | solution.py:180
  153.6 0.0 collective-permute-done.5.peer2
  153.6 3.6 %finish.6.rest_0_ = bf16[512,4096]{1,0:T(8,128)(2,1)} custom-call(s32[1]{0:T(128)} %bitcast.refs_1_.core, bf16[512,4096]{1,0:T(8,128)(2,1)S(1)} %copy-done.1, bf16[64,4096]{1,0:T(8,128)(2,1)S(1)} %fusion.8.own, bf16[64,4096]{1,0:T(8,128)(2,1)S(1)} %collective-permute-done.4.peer, ...), custom_call_target="tpu_custom_call", output_to_operand_aliasing={{}: (8, {})} | custom-call | flops 1024000000 | bytes 4194304 | tf_op jit(solution)/shard_map/finish/pallas_call | solution.py:180
  157.2 0.0 collective-permute-done.2.peer2
  157.2 2.8 %finish.7 = bf16[512,4096]{1,0:T(8,128)(2,1)} custom-call(s32[1]{0:T(128)} %bitcast.refs_1_.core, bf16[512,4096]{1,0:T(8,128)(2,1)S(1)} %copy-done.1, bf16[48,4096]{1,0:T(8,128)(2,1)S(1)} %fusion.10.own, bf16[48,4096]{1,0:T(8,128)(2,1)S(1)} %collective-permute-done.1.peer, ...), custom_call_target="tpu_custom_call", output_to_operand_aliasing={{}: (8, {})} | custom-call | flops 768000000 | bytes 3145728 | tf_op jit(solution)/shard_map/finish/pallas_call | solution.py:180
  (13 shorter events, 0.1 us)
Async XLA Ops:
  1.3 9.6 %copy-start = (bf16[512,4096]{1,0:T(8,128)(2,1)S(1)}, bf16[512,4096]{1,0:T(8,128)(2,1)}, u32[]{:S(2)}) copy-start(bf16[512,4096]{1,0:T(8,128)(2,1)} %hid.7) | copy-start | bytes 12582916
  1.3 9.6 %copy-start.6 = (bf16[4096,1024]{1,0:T(8,128)(2,1)S(1)}, bf16[4096,1024]{1,0:T(8,128)(2,1)}, u32[]{:S(2)}) copy-start(bf16[4096,1024]{1,0:T(8,128)(2,1)} %param.12) | copy-start | bytes 25165828
  10.6 4.9 %slice-start.2 = ((s8[8388608]{0:T(1024)(128)(4,1)}), s8[4194304]{0:T(1024)(128)(4,1)S(1)}, s32[]{:S(2)}) async-start(s8[8388608]{0:T(1024)(128)(4,1)} %bitcast.45), calls=%async_computation.2 | async-start | bytes 8388608
  10.9 4.6 %slice-start.3 = ((s8[8388608]{0:T(1024)(128)(4,1)}), s8[4194304]{0:T(1024)(128)(4,1)S(1)}, s32[]{:S(2)}) async-start(s8[8388608]{0:T(1024)(128)(4,1)} %bitcast.45), calls=%async_computation.3 | async-start | bytes 8388608
  15.6 13.4 %copy-start.4 = (f32[1024]{0:T(1024)S(1)}, f32[1024]{0:T(1024)}, u32[]{:S(2)}) copy-start(f32[1024]{0:T(1024)} %param.16) | copy-start | bytes 12292
  29.2 0.7 copy-start.5
  30.2 4.2 %slice-start = ((s8[8388608]{0:T(1024)(128)(4,1)}), s8[4194304]{0:T(1024)(128)(4,1)S(1)}, s32[]{:S(2)}) async-start(s8[8388608]{0:T(1024)(128)(4,1)} %bitcast.29), calls=%async_computation | async-start | bytes 8388608
  31.7 2.7 %slice-start.1 = ((s8[8388608]{0:T(1024)(128)(4,1)}), s8[4194304]{0:T(1024)(128)(4,1)S(1)}, s32[]{:S(2)}) async-start(s8[8388608]{0:T(1024)(128)(4,1)} %bitcast.29), calls=%async_computation.1 | async-start | bytes 8388608
  33.2 1.2 copy-start.3
  83.9 13.7 %collective-permute-start.3 = (bf16[2,64,4096]{2,1,0:T(8,128)(2,1)S(1)}, bf16[2,64,4096]{2,1,0:T(8,128)(2,1)S(1)}, u32[]{:S(2)}, u32[]{:S(2)}) collective-permute-start(bf16[2,64,4096]{2,1,0:T(8,128)(2,1)S(1)} %get-tuple-element.22.mine), channel_id=1, source_target_pairs={{0,1},{1,0},{2,3},{3,2},{4,5},{5,4},{6,7},{7,6}} | collective-permute-start | bytes 3145736 | tf_op jit(solution)/shard_map/ppermute | solution.py:236
  84.0 14.2 %collective-permute-start.9 = (bf16[2,80,4096]{2,1,0:T(8,128)(2,1)S(1)}, bf16[2,80,4096]{2,1,0:T(8,128)(2,1)S(1)}, u32[]{:S(2)}, u32[]{:S(2)}) collective-permute-start(bf16[2,80,4096]{2,1,0:T(8,128)(2,1)S(1)} %get-tuple-element.24.mine), channel_id=1, source_target_pairs={{0,1},{1,0},{2,3},{3,2},{4,5},{5,4},{6,7},{7,6}} | collective-permute-start | bytes 3932168 | tf_op jit(solution)/shard_map/ppermute | solution.py:236
  97.1 29.6 %collective-permute-start = (bf16[2,48,4096]{2,1,0:T(8,128)(2,1)S(1)}, bf16[2,48,4096]{2,1,0:T(8,128)(2,1)S(1)}, u32[]{:S(2)}, u32[]{:S(2)}) collective-permute-start(bf16[2,48,4096]{2,1,0:T(8,128)(2,1)S(1)} %get-tuple-element.21.mine), channel_id=1, source_target_pairs={{0,1},{1,0},{2,3},{3,2},{4,5},{5,4},{6,7},{7,6}} | collective-permute-start | bytes 2359304 | tf_op jit(solution)/shard_map/ppermute | solution.py:236
  97.2 3.7 %collective-permute-start.6 = (bf16[2,64,4096]{2,1,0:T(8,128)(2,1)S(1)}, bf16[2,64,4096]{2,1,0:T(8,128)(2,1)S(1)}, u32[]{:S(2)}, u32[]{:S(2)}) collective-permute-start(bf16[2,64,4096]{2,1,0:T(8,128)(2,1)S(1)} %get-tuple-element.23.mine), channel_id=1, source_target_pairs={{0,1},{1,0},{2,3},{3,2},{4,5},{5,4},{6,7},{7,6}} | collective-permute-start | bytes 3145736 | tf_op jit(solution)/shard_map/ppermute | solution.py:236
  97.8 47.6 %copy-start.1 = (bf16[512,4096]{1,0:T(8,128)(2,1)S(1)}, bf16[512,4096]{1,0:T(8,128)(2,1)}, u32[]{:S(2)}) copy-start(bf16[512,4096]{1,0:T(8,128)(2,1)} %hid.7) | copy-start | bytes 12582916
  97.8 47.6 %copy-start.2 = (f32[4096]{0:T(1024)S(1)}, f32[4096]{0:T(1024)}, u32[]{:S(2)}) copy-start(f32[4096]{0:T(1024)} %param.18) | copy-start | bytes 49156
  97.8 40.1 %collective-permute-start.4 = (bf16[64,4096]{1,0:T(8,128)(2,1)S(1)}, bf16[64,4096]{1,0:T(8,128)(2,1)S(1)}, u32[]{:S(2)}, u32[]{:S(2)}) collective-permute-start(bf16[64,4096]{1,0:T(8,128)(2,1)S(1)} %fusion.8.own), channel_id=1, source_target_pairs={{0,2},{2,0},{1,3},{3,1},{4,6},{6,4},{5,7},{7,5}} | collective-permute-start | bytes 1572872 | tf_op jit(solution)/shard_map/ppermute | solution.py:238
  98.4 28.3 %collective-permute-start.10 = (bf16[80,4096]{1,0:T(8,128)(2,1)S(1)}, bf16[80,4096]{1,0:T(8,128)(2,1)S(1)}, u32[]{:S(2)}, u32[]{:S(2)}) collective-permute-start(bf16[80,4096]{1,0:T(8,128)(2,1)S(1)} %fusion.7.own), channel_id=1, source_target_pairs={{0,2},{2,0},{1,3},{3,1},{4,6},{6,4},{5,7},{7,5}} | collective-permute-start | bytes 1966088 | tf_op jit(solution)/shard_map/ppermute | solution.py:238
  101.1 36.9 %collective-permute-start.7 = (bf16[64,4096]{1,0:T(8,128)(2,1)S(1)}, bf16[64,4096]{1,0:T(8,128)(2,1)S(1)}, u32[]{:S(2)}, u32[]{:S(2)}) collective-permute-start(bf16[64,4096]{1,0:T(8,128)(2,1)S(1)} %fusion.9.own), channel_id=1, source_target_pairs={{0,2},{2,0},{1,3},{3,1},{4,6},{6,4},{5,7},{7,5}} | collective-permute-start | bytes 1572872 | tf_op jit(solution)/shard_map/ppermute | solution.py:238
  126.7 18.7 %collective-permute-start.11 = (bf16[80,4096]{1,0:T(8,128)(2,1)S(1)}, bf16[80,4096]{1,0:T(8,128)(2,1)S(1)}, u32[]{:S(2)}, u32[]{:S(2)}) collective-permute-start(bf16[80,4096]{1,0:T(8,128)(2,1)S(1)} %collective-permute-done.10.peer), channel_id=1, source_target_pairs={{0,1},{1,0},{2,3},{3,2},{4,5},{5,4},{6,7},{7,6}} | collective-permute-start | bytes 1966088 | tf_op jit(solution)/shard_map/ppermute | solution.py:239
  126.8 18.6 %collective-permute-start.1 = (bf16[48,4096]{1,0:T(8,128)(2,1)S(1)}, bf16[48,4096]{1,0:T(8,128)(2,1)S(1)}, u32[]{:S(2)}, u32[]{:S(2)}) collective-permute-start(bf16[48,4096]{1,0:T(8,128)(2,1)S(1)} %fusion.10.own), channel_id=1, source_target_pairs={{0,2},{2,0},{1,3},{3,1},{4,6},{6,4},{5,7},{7,5}} | collective-permute-start | bytes 1179656 | tf_op jit(solution)/shard_map/ppermute | solution.py:238
  137.9 12.0 %collective-permute-start.8 = (bf16[64,4096]{1,0:T(8,128)(2,1)S(1)}, bf16[64,4096]{1,0:T(8,128)(2,1)S(1)}, u32[]{:S(2)}, u32[]{:S(2)}) collective-permute-start(bf16[64,4096]{1,0:T(8,128)(2,1)S(1)} %collective-permute-done.7.peer), channel_id=1, source_target_pairs={{0,1},{1,0},{2,3},{3,2},{4,5},{5,4},{6,7},{7,6}} | collective-permute-start | bytes 1572872 | tf_op jit(solution)/shard_map/ppermute | solution.py:239
  137.9 15.6 %collective-permute-start.5 = (bf16[64,4096]{1,0:T(8,128)(2,1)S(1)}, bf16[64,4096]{1,0:T(8,128)(2,1)S(1)}, u32[]{:S(2)}, u32[]{:S(2)}) collective-permute-start(bf16[64,4096]{1,0:T(8,128)(2,1)S(1)} %collective-permute-done.4.peer), channel_id=1, source_target_pairs={{0,1},{1,0},{2,3},{3,2},{4,5},{5,4},{6,7},{7,6}} | collective-permute-start | bytes 1572872 | tf_op jit(solution)/shard_map/ppermute | solution.py:239
  145.4 11.8 %collective-permute-start.2 = (bf16[48,4096]{1,0:T(8,128)(2,1)S(1)}, bf16[48,4096]{1,0:T(8,128)(2,1)S(1)}, u32[]{:S(2)}, u32[]{:S(2)}) collective-permute-start(bf16[48,4096]{1,0:T(8,128)(2,1)S(1)} %collective-permute-done.1.peer), channel_id=1, source_target_pairs={{0,1},{1,0},{2,3},{3,2},{4,5},{5,4},{6,7},{7,6}} | collective-permute-start | bytes 1179656 | tf_op jit(solution)/shard_map/ppermute | solution.py:239
